TPU v7x, 256 devices: a whole 4x4x8 slice. The times are simulated.
256 devices in a mesh: box: 256 (over y, z, x, core).
Axes of the slice: x: 4, y: 4, z: 8, core: 2. Of those that a mesh axis runs over, the one named last changes fastest.
Arguments:
- basis_vector: float32 [16, 1048576], P(None, 'box'), may hold values from -600 to 600
- diagonal: float32 [1048576], P('box'), may hold values from 0.25 to 2
- coords: int32 [2, 1048576], P(None, 'box'), may hold values from 0 to 4095
- phase_scale: int32 [1], replicated, may hold values from 1 to 8190
- sketch_rows: int32 [1048576], P('box'), may hold values from 0 to 2047
- sketch_signs: int32 [1048576], P('box'), may hold values from 0 to 1
Outputs:
- new_basis: float32 [16, 1048576], P(None, 'box')
- sketch: float32 [16, 2048], replicated
- arnoldi: float32 [2, 16], replicated
All inputs are finite; a program needn't handle non-finite values.
Results may differ from a plain program's by a relative error of at most 0.00019.
Values sent between devices are 32-bit elements; how exact they have to be, the bound alone decides.
A program may use at most 64 MiB of HBM per device.

v0:
```python
import functools
import math

import jax
import jax.numpy as jnp
from jax import lax
from jax.sharding import Mesh
from jax.sharding import PartitionSpec as P

RANK = 16
WIDTH = 32
LEAF = 32
SKETCH = 2048
BOX = ("box_0", "box_1", "box_2", "box_3")


modulus = 8191
epsilon = 1e-06


def swapped(x, axis, bit):
    return lax.ppermute(x, axis, [(i, i ^ 1 << bit) for i in range(lax.axis_size(axis))])


def one_axis_at_a_time(x, axes):
    return functools.reduce(lax.psum, axes, x)


def leaf_table(coords, phase_scale):
    scale_mod = phase_scale[0] % modulus
    freq = jnp.arange(RANK, dtype=jnp.int32)
    freq_first = freq % 4 + 1
    freq_second = freq // 4 + 1
    linear = (
        freq_first[:, None] * coords[0][None, :] + freq_second[:, None] * coords[1][None, :]
    ) % modulus
    phase = scale_mod * linear % modulus
    angle = phase.astype(jnp.float32) * (2.0 * math.pi / modulus)
    return jnp.concatenate([jnp.cos(angle), jnp.sin(angle)], 0) * (1.0 / math.sqrt(LEAF))


def translations(box_ids, segment_num, phase_scale):
    scale_mod = phase_scale[0] % modulus
    base_key = (box_ids * 37 + 101 * segment_num) % (modulus - 1) + 1
    unit_phase = scale_mod * base_key % modulus
    indices = jnp.arange(WIDTH, dtype=jnp.int32)
    prod_a = (indices[:, None] + 1) * (indices[None, :] + 2) % modulus
    prod_b = (indices[:, None] + 3) * (indices[None, :] + 1) % modulus
    phase_a = prod_a[:, :, None] * unit_phase[None, None, :] % modulus
    phase_b = (prod_b[:, :, None] * unit_phase[None, None, :] + 4096) % modulus
    factor = 2.0 * math.pi / modulus
    ident = jnp.eye(WIDTH, dtype=jnp.float32)[:, :, None]
    own_map = 0.85 * ident + 0.35 / math.sqrt(WIDTH) * jnp.cos(phase_a.astype(jnp.float32) * factor)
    cross_map = 0.6 / math.sqrt(WIDTH) * jnp.cos(phase_b.astype(jnp.float32) * factor)
    return (own_map, cross_map)


def mix(matrix, coeffs):
    return jnp.einsum("wvg,vgq->wgq", matrix, coeffs, precision=lax.Precision.HIGHEST)


def one_segment(coeffs, segment_num, group_boxes, phase_scale):
    own_map, cross_map = translations(group_boxes, segment_num, phase_scale)
    partner = swapped(coeffs, BOX, segment_num)
    return mix(own_map, coeffs) + mix(cross_map, partner)


def body(basis_vector, diagonal, coords, phase_scale, sketch_rows, sketch_signs):
    highest = lax.Precision.HIGHEST
    columns, local_points = basis_vector.shape
    box_count = local_points // LEAF
    devices = lax.axis_size(BOX)
    segment_count = devices.bit_length() - 1
    rank_id = lax.axis_index(BOX)
    local_ids = jnp.arange(box_count, dtype=jnp.int32)
    group_boxes = rank_id * box_count + local_ids
    leaf_map = leaf_table(coords, phase_scale)
    leaf_boxes = leaf_map.reshape(WIDTH, box_count, LEAF)
    blocks = basis_vector.reshape(columns, box_count, LEAF)
    coeffs = jnp.einsum("wgs,qgs->wgq", leaf_boxes, blocks, precision=highest)
    for segment_num in range(segment_count):
        coeffs = one_segment(coeffs, segment_num, group_boxes, phase_scale)
    applied = jnp.einsum("wgs,wgq->qgs", leaf_boxes, coeffs, precision=highest).reshape(
        columns, local_points
    )
    image = diagonal[None, :] * basis_vector + applied
    total_points = local_points * devices
    sketch_factor = math.sqrt(SKETCH / total_points)
    sign_values = (2 * sketch_signs - 1).astype(jnp.float32)
    block_rows = math.gcd(local_points, 512)
    block_count = local_points // block_rows
    row_blocks = sketch_rows.reshape(block_count, block_rows)
    sketch_ids = jnp.arange(SKETCH, dtype=jnp.int32)
    inner_sum, square_sum = (
        one_axis_at_a_time(jnp.sum(basis_vector * image, axis=1), BOX),
        one_axis_at_a_time(jnp.sum(basis_vector * basis_vector, axis=1), BOX),
    )
    projection = inner_sum / total_points / (square_sum / total_points + epsilon)
    residual = image - projection[:, None] * basis_vector
    energy_sum = one_axis_at_a_time(jnp.sum(residual * residual, axis=1), BOX)
    spread = jnp.sqrt(energy_sum / total_points + epsilon)
    new_basis = residual / spread[:, None]
    signed = (new_basis * sign_values[None, :]).reshape(columns, block_count, block_rows)
    signed = jnp.transpose(signed, (1, 0, 2))

    def add_block(total, pieces):
        piece, rows_here = pieces
        onehot = (rows_here[:, None] == sketch_ids[None, :]).astype(jnp.float32)
        return (
            total + jnp.dot(piece, onehot, precision=highest, preferred_element_type=jnp.float32),
            None,
        )

    total, unused = lax.scan(
        add_block, jnp.zeros((columns, SKETCH), jnp.float32), (signed, row_blocks)
    )
    sketch = lax.psum(total, BOX) * sketch_factor
    arnoldi = jnp.stack([projection, spread])
    return (new_basis, sketch, arnoldi)


def solution(mesh):
    torus = Mesh(mesh.devices.reshape(4, 8, 4, 2), ("box_0", "box_1", "box_2", "box_3"))
    placed = (P(None, BOX), P(BOX), P(None, BOX), P(), P(BOX), P(BOX))
    return jax.shard_map(
        body, mesh=torus, in_specs=placed, out_specs=(P(None, BOX), P(), P()), check_vma=False
    )
```

profile of v0, /device:TPU:1, one launch (start us, length us, event | category | flops | bytes accessed | tf_op | source)
XLA Modules:
  0.0 642.4 jit_solution(368438935068808877)
XLA Ops:
  13.7 5.1 fusion.180
  20.0 3.6 collective-permute-start
  33.5 14.7 %fusion.13 = f32[128,16,32]{2,1,0:T(8,128)} fusion(f32[32,128,16]{0,2,1:T(8,128)S(1)} %fusion.180, s32[128]{0:T(128)} %and_select_fusion.14, s32[32,32]{1,0:T(8,128)S(1)} %get-tuple-element.75, f32[32,32]{1,0:T(8,128)} %fusion.364), kind=kOutput, calls=%fused_computation.30 | convolution fusion | flops 26607616 | bytes 532992 | tf_op jit(solution)/shard_map/wvg,vgq->wgq/dot_general | solution.py:59
  48.2 2.4 copy.19
  50.6 13.4 %fusion.231 = f32[32,128,16]{0,2,1:T(8,128)S(1)} fusion(f32[128,16,32]{2,1,0:T(8,128)} %fusion.13, f32[32,128,16]{0,2,1:T(8,128)} %copy.19, s32[32,32]{1,0:T(8,128)} %get-tuple-element.74, s32[128]{0:T(128)} %and_select_fusion.14), kind=kOutput, calls=%fused_computation.198 | convolution fusion | flops 26673152 | bytes 791040 | tf_op jit(solution)/shard_map/wvg,vgq->wgq/dot_general | solution.py:59
  65.1 14.7 %fusion.26 = f32[128,16,32]{2,1,0:T(8,128)} fusion(f32[32,128,16]{0,2,1:T(8,128)S(1)} %fusion.231, s32[128]{0:T(128)} %and_select_fusion.12, s32[32,32]{1,0:T(8,128)} %copy-done.3, f32[32,32]{1,0:T(8,128)} %fusion.364), kind=kOutput, calls=%fused_computation.41 | convolution fusion | flops 26607616 | bytes 532992 | tf_op jit(solution)/shard_map/wvg,vgq->wgq/dot_general | solution.py:59
  82.2 13.3 %fusion.225 = f32[32,128,16]{0,2,1:T(8,128)S(1)} fusion(f32[128,16,32]{2,1,0:T(8,128)} %fusion.26, f32[32,128,16]{0,2,1:T(8,128)} %copy.21, s32[128]{0:T(128)} %and_select_fusion.12, s32[32,32]{1,0:T(8,128)} %get-tuple-element.74), kind=kOutput, calls=%fused_computation.196 | convolution fusion | flops 26673152 | bytes 791040 | tf_op jit(solution)/shard_map/wvg,vgq->wgq/dot_general | solution.py:59
  98.9 14.7 %fusion.39 = f32[128,16,32]{2,1,0:T(8,128)} fusion(f32[32,128,16]{0,2,1:T(8,128)S(1)} %fusion.225, s32[128]{0:T(128)} %and_select_fusion.10, s32[32,32]{1,0:T(8,128)} %copy-done.3, f32[32,32]{1,0:T(8,128)} %fusion.364), kind=kOutput, calls=%fused_computation.52 | convolution fusion | flops 26607616 | bytes 532992 | tf_op jit(solution)/shard_map/wvg,vgq->wgq/dot_general | solution.py:59
  116.0 13.3 %fusion.219 = f32[32,128,16]{0,2,1:T(8,128)S(1)} fusion(f32[128,16,32]{2,1,0:T(8,128)} %fusion.39, f32[32,128,16]{0,2,1:T(8,128)} %copy.23, s32[128]{0:T(128)} %and_select_fusion.10, s32[32,32]{1,0:T(8,128)} %get-tuple-element.74), kind=kOutput, calls=%fused_computation.194 | convolution fusion | flops 26673152 | bytes 791040 | tf_op jit(solution)/shard_map/wvg,vgq->wgq/dot_general | solution.py:59
  132.1 14.7 %fusion.52 = f32[128,16,32]{2,1,0:T(8,128)} fusion(f32[32,128,16]{0,2,1:T(8,128)S(1)} %fusion.219, s32[128]{0:T(128)} %and_select_fusion.8, s32[32,32]{1,0:T(8,128)} %copy-done.3, f32[32,32]{1,0:T(8,128)} %fusion.364), kind=kOutput, calls=%fused_computation.63 | convolution fusion | flops 26607616 | bytes 532992 | tf_op jit(solution)/shard_map/wvg,vgq->wgq/dot_general | solution.py:59
  149.2 13.3 %fusion.213 = f32[32,128,16]{0,2,1:T(8,128)S(1)} fusion(f32[128,16,32]{2,1,0:T(8,128)} %fusion.52, f32[32,128,16]{0,2,1:T(8,128)} %copy.25, s32[128]{0:T(128)} %and_select_fusion.8, s32[32,32]{1,0:T(8,128)} %get-tuple-element.74), kind=kOutput, calls=%fused_computation.192 | convolution fusion | flops 26673152 | bytes 791040 | tf_op jit(solution)/shard_map/wvg,vgq->wgq/dot_general | solution.py:59
  163.7 3.4 collective-permute-start.4
  167.1 14.7 %fusion.65 = f32[128,16,32]{2,1,0:T(8,128)} fusion(f32[32,128,16]{0,2,1:T(8,128)S(1)} %fusion.213, s32[128]{0:T(128)} %and_select_fusion.6, s32[32,32]{1,0:T(8,128)} %copy-done.3, f32[32,32]{1,0:T(8,128)} %fusion.364), kind=kOutput, calls=%fused_computation.74 | convolution fusion | flops 26607616 | bytes 532992 | tf_op jit(solution)/shard_map/wvg,vgq->wgq/dot_general | solution.py:59
  184.2 13.3 %fusion.207 = f32[32,128,16]{0,2,1:T(8,128)S(1)} fusion(f32[128,16,32]{2,1,0:T(8,128)} %fusion.65, f32[32,128,16]{0,2,1:T(8,128)} %copy.27, s32[128]{0:T(128)} %and_select_fusion.6, s32[32,32]{1,0:T(8,128)} %get-tuple-element.74), kind=kOutput, calls=%fused_computation.190 | convolution fusion | flops 26673152 | bytes 791040 | tf_op jit(solution)/shard_map/wvg,vgq->wgq/dot_general | solution.py:59
  198.7 4.2 collective-permute-start.5
  202.9 14.7 %fusion.78 = f32[128,16,32]{2,1,0:T(8,128)} fusion(f32[32,128,16]{0,2,1:T(8,128)S(1)} %fusion.207, s32[128]{0:T(128)} %and_select_fusion.4, s32[32,32]{1,0:T(8,128)} %copy-done.3, f32[32,32]{1,0:T(8,128)} %fusion.364), kind=kOutput, calls=%fused_computation.85 | convolution fusion | flops 26607616 | bytes 532992 | tf_op jit(solution)/shard_map/wvg,vgq->wgq/dot_general | solution.py:59
  220.0 13.3 %fusion.201 = f32[32,128,16]{0,2,1:T(8,128)S(1)} fusion(f32[128,16,32]{2,1,0:T(8,128)} %fusion.78, f32[32,128,16]{0,2,1:T(8,128)} %copy.29, s32[128]{0:T(128)} %and_select_fusion.4, s32[32,32]{1,0:T(8,128)} %get-tuple-element.74), kind=kOutput, calls=%fused_computation.188 | convolution fusion | flops 26673152 | bytes 791040 | tf_op jit(solution)/shard_map/wvg,vgq->wgq/dot_general | solution.py:59
  236.0 14.7 %fusion.91 = f32[128,16,32]{2,1,0:T(8,128)} fusion(f32[32,128,16]{0,2,1:T(8,128)S(1)} %fusion.201, s32[128]{0:T(128)} %and_select_fusion.2, s32[32,32]{1,0:T(8,128)} %copy-done.3, f32[32,32]{1,0:T(8,128)} %fusion.364), kind=kOutput, calls=%fused_computation.96 | convolution fusion | flops 26607616 | bytes 532992 | tf_op jit(solution)/shard_map/wvg,vgq->wgq/dot_general | solution.py:59
  253.1 13.3 %fusion.195 = f32[32,128,16]{0,2,1:T(8,128)S(1)} fusion(f32[128,16,32]{2,1,0:T(8,128)} %fusion.91, f32[32,128,16]{0,2,1:T(8,128)} %copy.31, s32[128]{0:T(128)} %and_select_fusion.2, s32[32,32]{1,0:T(8,128)} %get-tuple-element.74), kind=kOutput, calls=%fused_computation.186 | convolution fusion | flops 26673152 | bytes 791040 | tf_op jit(solution)/shard_map/wvg,vgq->wgq/dot_general | solution.py:59
  267.6 2.6 collective-permute-start.7
  270.2 14.7 %fusion.104 = f32[128,16,32]{2,1,0:T(8,128)} fusion(f32[32,128,16]{0,2,1:T(8,128)S(1)} %fusion.195, s32[128]{0:T(128)} %and_select_fusion, s32[32,32]{1,0:T(8,128)} %copy-done.3, f32[32,32]{1,0:T(8,128)} %fusion.364), kind=kOutput, calls=%fused_computation.107 | convolution fusion | flops 26607616 | bytes 532992 | tf_op jit(solution)/shard_map/wvg,vgq->wgq/dot_general | solution.py:59
  286.4 14.2 %fusion.189 = f32[32,128,16]{0,2,1:T(8,128)S(1)} fusion(f32[128,16,32]{2,1,0:T(8,128)} %fusion.104, f32[32,128,16]{0,2,1:T(8,128)S(1)} %copy.33, s32[128]{0:T(128)} %and_select_fusion, s32[32,32]{1,0:T(8,128)} %get-tuple-element.74), kind=kOutput, calls=%fused_computation.184 | convolution fusion | flops 26673152 | bytes 791040 | tf_op jit(solution)/shard_map/wvg,vgq->wgq/dot_general | solution.py:59
  303.8 6.0 all-reduce.2
  309.8 11.4 %all-reduce = (f32[16]{0:T(128)S(1)}, f32[16]{0:T(128)S(1)}) all-reduce(f32[16]{0:T(128)S(1)} %get-tuple-element.64, f32[16]{0:T(128)S(1)} %get-tuple-element.65), channel_id=1, replica_groups=mesh['box_0'=4,'box_1'=8,'box_2'=4,'box_3'=2] {'box_1'}, use_global_device_ids=true, to_apply=%region_7.8 | all-reduce | flops 32 | bytes 256 | tf_op jit(solution)/shard_map/psum | solution.py:26
  321.2 6.2 all-reduce.1
  327.3 11.8 %all-reduce.3 = (f32[16]{0:T(128)S(1)}, f32[16]{0:T(128)S(1)}) all-reduce(f32[16]{0:T(128)S(1)} %get-tuple-element.62, f32[16]{0:T(128)S(1)} %get-tuple-element.63), channel_id=1, replica_groups=mesh['box_0'=4,'box_1'=8,'box_2'=4,'box_3'=2] {'box_3'}, use_global_device_ids=true, to_apply=%region_9.10 | all-reduce | flops 32 | bytes 256 | tf_op jit(solution)/shard_map/psum | solution.py:26
  339.4 7.5 %psum.99 = f32[16]{0:T(128)S(1)} all-reduce(f32[16]{0:T(128)S(1)} %multiply_reduce_fusion), channel_id=1, replica_groups=mesh['box_0'=4,'box_1'=8,'box_2'=4,'box_3'=2] {'box_0'}, use_global_device_ids=true, to_apply=%region_11.12 | all-reduce | flops 16 | bytes 128 | tf_op jit(solution)/shard_map/psum | solution.py:26
  346.9 11.4 %psum.100 = f32[16]{0:T(128)S(1)} all-reduce(f32[16]{0:T(128)S(1)} %psum.99), channel_id=1, replica_groups=mesh['box_0'=4,'box_1'=8,'box_2'=4,'box_3'=2] {'box_1'}, use_global_device_ids=true, to_apply=%region_12.13 | all-reduce | flops 16 | bytes 128 | tf_op jit(solution)/shard_map/psum | solution.py:26
  358.3 7.2 %psum.101 = f32[16]{0:T(128)S(1)} all-reduce(f32[16]{0:T(128)S(1)} %psum.100), channel_id=1, replica_groups=mesh['box_0'=4,'box_1'=8,'box_2'=4,'box_3'=2] {'box_2'}, use_global_device_ids=true, to_apply=%region_13.14 | all-reduce | flops 16 | bytes 128 | tf_op jit(solution)/shard_map/psum | solution.py:26
  365.5 10.2 %psum.102 = f32[16]{0:T(128)S(1)} all-reduce(f32[16]{0:T(128)S(1)} %psum.101), channel_id=1, replica_groups=mesh['box_0'=4,'box_1'=8,'box_2'=4,'box_3'=2] {'box_3'}, use_global_device_ids=true, to_apply=%region_14.15 | all-reduce | flops 16 | bytes 128 | tf_op jit(solution)/shard_map/psum | solution.py:26
  376.6 17.6 %while.11 = (s32[]{:T(128)}, f32[16,2048]{1,0:T(8,128)S(1)}, f32[8,16,512]{2,1,0:T(8,128)S(1)}, s32[8,512]{1,0:T(8,128)}, s32[]{:T(128)}, /*index=5*/s32[]{:T(128)}) while((s32[]{:T(128)}, f32[16,2048]{1,0:T(8,128)S(1)}, f32[8,16,512]{2,1,0:T(8,128)S(1)}, s32[8,512]{1,0:T(8,128)}, s32[]{:T(128)}, /*index=5*/s32[]{:T(128)}) %tuple.39), condition=%wide.region_16.17_spmd.clone, body=%wide.region_15.16_spmd.clone.sunk | while | flops 202440704 | bytes 301151 | solution.py:114
  395.5 238.3 %all-reduce.6.cloned.1.call-done = f32[16,2048]{1,0:T(8,128)} async-done(((f32[16,2048]{1,0:T(8,128)}), f32[16,2048]{1,0:T(8,128)}) %all-reduce.6.cloned.1.call-update) | async-done | bytes 131088 | tf_op jit(solution)/shard_map/psum | solution.py:117
  (89 shorter events, 70.9 us)
Async XLA Ops:
  7.2 626.6 %all-reduce.6.cloned.1.call-start = ((), (), s32[]{:S(2)}) async-start(), calls=%async_computation | async-start | bytes 262144 | tf_op jit(solution)/shard_map/psum | solution.py:117
  9.1 3.3 copy-start
  20.0 28.2 %collective-permute-start = (f32[32,128,16]{1,2,0:T(8,128)}, f32[32,128,16]{1,2,0:T(8,128)}, u32[]{:S(2)}, u32[]{:S(2)}) collective-permute-start(f32[32,128,16]{1,2,0:T(8,128)} %copy.18), channel_id=1, source_target_pairs={{0,1},{1,0},{2,3},{3,2},{4,5},{5,4},{6,7},{7,6},{8,9},{9,8},{10,11... | collective-permute-start | bytes 786440 | tf_op jit(solution)/shard_map/ppermute | solution.py:22
  33.5 14.7 %copy-start.3 = (s32[32,32]{1,0:T(8,128)}, s32[32,32]{1,0:T(8,128)S(1)}, u32[]{:S(2)}) copy-start(s32[32,32]{1,0:T(8,128)S(1)} %get-tuple-element.75) | copy-start | bytes 12292
  65.1 14.7 %collective-permute-start.1 = (f32[32,128,16]{1,2,0:T(8,128)}, f32[32,128,16]{1,2,0:T(8,128)}, u32[]{:S(2)}, u32[]{:S(2)}) collective-permute-start(f32[32,128,16]{1,2,0:T(8,128)} %copy.20), channel_id=1, source_target_pairs={{0,2},{1,3},{2,0},{3,1},{4,6},{5,7},{6,4},{7,5},{8,10},{9,11},{10,... | collective-permute-start | bytes 786440 | tf_op jit(solution)/shard_map/ppermute | solution.py:22
  96.8 16.8 %collective-permute-start.2 = (f32[32,128,16]{1,2,0:T(8,128)}, f32[32,128,16]{1,2,0:T(8,128)}, u32[]{:S(2)}, u32[]{:S(2)}) collective-permute-start(f32[32,128,16]{1,2,0:T(8,128)} %copy.22), channel_id=1, source_target_pairs={{0,4},{1,5},{2,6},{3,7},{4,0},{5,1},{6,2},{7,3},{8,12},{9,13},{10,... | collective-permute-start | bytes 786440 | tf_op jit(solution)/shard_map/ppermute | solution.py:22
  130.5 16.3 %collective-permute-start.3 = (f32[32,128,16]{1,2,0:T(8,128)}, f32[32,128,16]{1,2,0:T(8,128)}, u32[]{:S(2)}, u32[]{:S(2)}) collective-permute-start(f32[32,128,16]{1,2,0:T(8,128)} %copy.24), channel_id=1, source_target_pairs={{0,8},{1,9},{2,10},{3,11},{4,12},{5,13},{6,14},{7,15},{8,0},{9,1},... | collective-permute-start | bytes 786440 | tf_op jit(solution)/shard_map/ppermute | solution.py:22
  163.7 18.1 %collective-permute-start.4 = (f32[32,128,16]{1,2,0:T(8,128)}, f32[32,128,16]{1,2,0:T(8,128)}, u32[]{:S(2)}, u32[]{:S(2)}) collective-permute-start(f32[32,128,16]{1,2,0:T(8,128)} %copy.26), channel_id=1, source_target_pairs={{0,16},{1,17},{2,18},{3,19},{4,20},{5,21},{6,22},{7,23},{8,24},{9,... | collective-permute-start | bytes 786440 | tf_op jit(solution)/shard_map/ppermute | solution.py:22
  198.7 18.9 %collective-permute-start.5 = (f32[32,128,16]{1,2,0:T(8,128)}, f32[32,128,16]{1,2,0:T(8,128)}, u32[]{:S(2)}, u32[]{:S(2)}) collective-permute-start(f32[32,128,16]{1,2,0:T(8,128)} %copy.28), channel_id=1, source_target_pairs={{0,32},{1,33},{2,34},{3,35},{4,36},{5,37},{6,38},{7,39},{8,40},{9,... | collective-permute-start | bytes 786440 | tf_op jit(solution)/shard_map/ppermute | solution.py:22
  234.6 16.1 %collective-permute-start.6 = (f32[32,128,16]{1,2,0:T(8,128)}, f32[32,128,16]{1,2,0:T(8,128)}, u32[]{:S(2)}, u32[]{:S(2)}) collective-permute-start(f32[32,128,16]{1,2,0:T(8,128)} %copy.30), channel_id=1, source_target_pairs={{0,64},{1,65},{2,66},{3,67},{4,68},{5,69},{6,70},{7,71},{8,72},{9,... | collective-permute-start | bytes 786440 | tf_op jit(solution)/shard_map/ppermute | solution.py:22
  267.6 17.3 %collective-permute-start.7 = (f32[32,128,16]{1,2,0:T(8,128)}, f32[32,128,16]{1,2,0:T(8,128)}, u32[]{:S(2)}, u32[]{:S(2)}) collective-permute-start(f32[32,128,16]{1,2,0:T(8,128)} %copy.32), channel_id=1, source_target_pairs={{0,128},{1,129},{2,130},{3,131},{4,132},{5,133},{6,134},{7,135},{8... | collective-permute-start | bytes 786440 | tf_op jit(solution)/shard_map/ppermute | solution.py:22
  302.7 0.9 copy-start.1
  394.2 0.7 copy-start.2
Sparse Core Ops, SparseCore 0:
  395.0 238.7 all-reduce.5
where the time goes:
time: 651 us; the launch traced here: 642 us
  matrix products  244 us (37%)
  waiting for transfers between devices  238 us (37%)
  blocking collectives  71.8 us (11%)
  local copies, waits for them, and re-layouts  40.7 us (6%)
  starting transfers between devices  19.1 us (3%)
  between operations  15.1 us (2%)
  other arithmetic  13.4 us (2%)
    psum x1, waiting for transfers between devices, body(): sketch = lax.psum(total, BOX) * sketch_factor  238 us
    dot_general x16, matrix products, mix(): jnp.einsum('wvg,vgq->wgq', matrix, coeffs, precision=lax.Precision.HIGHEST)  225 us
    psum x8, blocking collectives, one_axis_at_a_time(): return functools.reduce(lax.psum, axes, x)  71.8 us
    ppermute x8, starting transfers between devices, swapped(): lax.ppermute(x, axis, [(i, i ^ 1 << bit) for i in range(lax.axis_size(axi...  19 us
    ppermute x8, local copies, waits for them, and re-layouts, swapped(): lax.ppermute(x, axis, [(i, i ^ 1 << bit) for i in range(lax.axis_size(axi...  18.3 us
  transfers between devices with their start and end apart: 9, of which 1 were waited for; matrix products, arithmetic and copies ran while one was open for 20% of the time, Pallas kernels for 0%

commit v1 on v0

--- a/solution.py
+++ b/solution.py
@@ -4,14 +4,15 @@
 import jax
 import jax.numpy as jnp
 from jax import lax
-from jax.sharding import Mesh
+from jax.experimental import pallas as pl
+from jax.experimental.pallas import tpu as pltpu
 from jax.sharding import PartitionSpec as P
 
 RANK = 16
 WIDTH = 32
 LEAF = 32
 SKETCH = 2048
-BOX = ("box_0", "box_1", "box_2", "box_3")
+BOX = "box"
 
 
 modulus = 8191
@@ -23,7 +24,80 @@
 
 
 def one_axis_at_a_time(x, axes):
-    return functools.reduce(lax.psum, axes, x)
+    return lax.psum(x, axes)
+
+
+def all_sum_kernel(devices, x_ref, o_ref, parts, chunk, gathered, send_sem, recv_sem, gather_send, gather_recv):
+    me = lax.axis_index(BOX)
+    peers = devices - 1
+    barrier = pltpu.get_barrier_semaphore()
+
+    def peer(step):
+        return lax.rem(me + step + 1, devices)
+
+    def greet(step, carry):
+        pl.semaphore_signal(barrier, inc=1, device_id=(peer(step),), device_id_type=pl.DeviceIdType.MESH)
+        return carry
+
+    lax.fori_loop(0, peers, greet, 0)
+    pl.semaphore_wait(barrier, peers)
+
+    def scatter(step, carry):
+        to = peer(step)
+        pltpu.make_async_remote_copy(
+            src_ref=x_ref.at[pl.ds(to, 1)],
+            dst_ref=parts.at[pl.ds(me, 1)],
+            send_sem=send_sem,
+            recv_sem=recv_sem,
+            device_id=(to,),
+            device_id_type=pl.DeviceIdType.MESH,
+        ).start()
+        return carry
+
+    lax.fori_loop(0, peers, scatter, 0)
+    parts[pl.ds(me, 1)] = x_ref[pl.ds(me, 1)]
+    pltpu.make_async_copy(parts.at[pl.ds(0, peers)], parts.at[pl.ds(0, peers)], recv_sem).wait()
+    chunk[...] = jnp.sum(parts[...], axis=0, keepdims=True)
+
+    def gather(step, carry):
+        to = peer(step)
+        pltpu.make_async_remote_copy(
+            src_ref=chunk,
+            dst_ref=gathered.at[pl.ds(me, 1)],
+            send_sem=gather_send,
+            recv_sem=gather_recv,
+            device_id=(to,),
+            device_id_type=pl.DeviceIdType.MESH,
+        ).start()
+        return carry
+
+    lax.fori_loop(0, peers, gather, 0)
+    gathered[pl.ds(me, 1)] = chunk[...]
+    for done in (gather_recv, gather_send, send_sem):
+        pltpu.make_async_copy(gathered.at[pl.ds(0, peers)], gathered.at[pl.ds(0, peers)], done).wait()
+    o_ref[...] = gathered[...]
+
+
+def all_sum(x, devices):
+    rows = x.shape[0] * x.shape[1] // devices
+    flat = x.reshape(devices, rows)
+    call = pl.pallas_call(
+        functools.partial(all_sum_kernel, devices),
+        out_shape=jax.ShapeDtypeStruct(flat.shape, jnp.float32),
+        in_specs=[pl.BlockSpec(memory_space=pltpu.VMEM)],
+        out_specs=pl.BlockSpec(memory_space=pltpu.VMEM),
+        scratch_shapes=[
+            pltpu.VMEM(flat.shape, jnp.float32),
+            pltpu.VMEM((1, rows), jnp.float32),
+            pltpu.VMEM(flat.shape, jnp.float32),
+            pltpu.SemaphoreType.DMA,
+            pltpu.SemaphoreType.DMA,
+            pltpu.SemaphoreType.DMA,
+            pltpu.SemaphoreType.DMA,
+        ],
+        compiler_params=pltpu.CompilerParams(collective_id=1, has_side_effects=True),
+    )
+    return call(flat).reshape(x.shape)
 
 
 def leaf_table(coords, phase_scale):
@@ -114,14 +188,13 @@
     total, unused = lax.scan(
         add_block, jnp.zeros((columns, SKETCH), jnp.float32), (signed, row_blocks)
     )
-    sketch = lax.psum(total, BOX) * sketch_factor
+    sketch = all_sum(total, devices) * sketch_factor
     arnoldi = jnp.stack([projection, spread])
     return (new_basis, sketch, arnoldi)
 
 
 def solution(mesh):
-    torus = Mesh(mesh.devices.reshape(4, 8, 4, 2), ("box_0", "box_1", "box_2", "box_3"))
     placed = (P(None, BOX), P(BOX), P(None, BOX), P(), P(BOX), P(BOX))
     return jax.shard_map(
-        body, mesh=torus, in_specs=placed, out_specs=(P(None, BOX), P(), P()), check_vma=False
-    )
+        body, mesh=mesh, in_specs=placed, out_specs=(P(None, BOX), P(), P()), check_vma=False
+    )

time: 651 us -> 493 us (0.76)
  waiting for transfers between devices: 238 us -> 0.02 us
  blocking collectives: 71.8 us -> 147 us
  Pallas kernels: 0 us -> 27.5 us
  between operations: 15.1 us -> 1.88 us
    psum x1 -> x0, waiting for transfers between devices: 238 us -> none  [body(): sketch = lax.psum(total, BOX) * sketch_factor]
    psum x8 -> x2, blocking collectives: 71.8 us -> 147 us  [one_axis_at_a_time(): return lax.psum(x, axes)]
    pallas_call x0 -> x1, Pallas kernels: none -> 27.5 us  [all_sum(): return call(flat).reshape(x.shape)]
  transfers between devices with their start and end apart: 9 -> 8, of which waited for: 1 -> 0; matrix products, arithmetic and copies ran while one was open for 20% -> 26% of each run, Pallas kernels for 0% -> 0%
where the time goes in v1:
time: 493 us; the launch traced here: 486 us
  matrix products  244 us (49%)
  blocking collectives  147 us (30%)
  local copies, waits for them, and re-layouts  34.3 us (7%)
  Pallas kernels  27.5 us (6%)
  starting transfers between devices  18.8 us (4%)
  other arithmetic  12.5 us (3%)
    dot_general x16, matrix products, mix(): jnp.einsum('wvg,vgq->wgq', matrix, coeffs, precision=lax.Precision.HIGHEST)  225 us
    psum x2, blocking collectives, one_axis_at_a_time(): return lax.psum(x, axes)  147 us
    pallas_call x1, Pallas kernels, all_sum(): return call(flat).reshape(x.shape)  27.5 us
    ppermute x8, starting transfers between devices, swapped(): lax.ppermute(x, axis, [(i, i ^ 1 << bit) for i in range(lax.axis_size(axi...  18.8 us
    ppermute x8, local copies, waits for them, and re-layouts, swapped(): lax.ppermute(x, axis, [(i, i ^ 1 << bit) for i in range(lax.axis_size(axi...  18.3 us
    dot_general x8, matrix products, add_block(): jnp.dot(piece, onehot, precision=highest, preferred_element_type=jnp.floa...  11.8 us
  transfers between devices with their start and end apart: 8, of which 0 were waited for; matrix products, arithmetic and copies ran while one was open for 26% of the time, Pallas kernels for 0%

profile of v1, /device:TPU:1, one launch (start us, length us, event | category | flops | bytes accessed | tf_op | source)
XLA Modules:
  0.0 485.9 jit_solution(14689168861059528779)
XLA Ops:
  7.1 5.1 %fusion.180 = f32[32,128,16]{0,2,1:T(8,128)S(1)} fusion(f32[32,128,32]{2,0,1:T(8,128)S(1)} %copy.16, f32[16,128,32]{2,1,0:T(8,128)} %reshape.329), kind=kOutput, calls=%fused_computation.181 | convolution fusion | flops 25296896 | bytes 1048576 | tf_op jit(solution)/shard_map/wgs,qgs->wgq/dot_general | solution.py:154
  13.4 3.4 collective-permute-start
  25.1 14.7 %fusion.13 = f32[128,16,32]{2,1,0:T(8,128)} fusion(f32[32,128,16]{0,2,1:T(8,128)S(1)} %fusion.180, s32[128]{0:T(128)} %and_select_fusion.14, s32[32,32]{1,0:T(8,128)S(1)} %get-tuple-element.69, f32[32,32]{1,0:T(8,128)} %fusion.364), kind=kOutput, calls=%fused_computation.30 | convolution fusion | flops 26607616 | bytes 532992 | tf_op jit(solution)/shard_map/wvg,vgq->wgq/dot_general | solution.py:133
  39.8 2.4 copy.19
  42.2 13.4 %fusion.231 = f32[32,128,16]{0,2,1:T(8,128)S(1)} fusion(f32[128,16,32]{2,1,0:T(8,128)} %fusion.13, f32[32,128,16]{0,2,1:T(8,128)} %copy.19, s32[32,32]{1,0:T(8,128)} %get-tuple-element.68, s32[128]{0:T(128)} %and_select_fusion.14), kind=kOutput, calls=%fused_computation.198 | convolution fusion | flops 26673152 | bytes 791040 | tf_op jit(solution)/shard_map/wvg,vgq->wgq/dot_general | solution.py:133
  56.7 14.7 %fusion.26 = f32[128,16,32]{2,1,0:T(8,128)} fusion(f32[32,128,16]{0,2,1:T(8,128)S(1)} %fusion.231, s32[128]{0:T(128)} %and_select_fusion.12, s32[32,32]{1,0:T(8,128)} %copy-done.3, f32[32,32]{1,0:T(8,128)} %fusion.364), kind=kOutput, calls=%fused_computation.41 | convolution fusion | flops 26607616 | bytes 532992 | tf_op jit(solution)/shard_map/wvg,vgq->wgq/dot_general | solution.py:133
  71.4 2.4 copy.21
  73.8 13.3 %fusion.225 = f32[32,128,16]{0,2,1:T(8,128)S(1)} fusion(f32[128,16,32]{2,1,0:T(8,128)} %fusion.26, f32[32,128,16]{0,2,1:T(8,128)} %copy.21, s32[128]{0:T(128)} %and_select_fusion.12, s32[32,32]{1,0:T(8,128)} %get-tuple-element.68), kind=kOutput, calls=%fused_computation.196 | convolution fusion | flops 26673152 | bytes 791040 | tf_op jit(solution)/shard_map/wvg,vgq->wgq/dot_general | solution.py:133
  90.7 14.7 %fusion.39 = f32[128,16,32]{2,1,0:T(8,128)} fusion(f32[32,128,16]{0,2,1:T(8,128)S(1)} %fusion.225, s32[128]{0:T(128)} %and_select_fusion.10, s32[32,32]{1,0:T(8,128)} %copy-done.3, f32[32,32]{1,0:T(8,128)} %fusion.364), kind=kOutput, calls=%fused_computation.52 | convolution fusion | flops 26607616 | bytes 532992 | tf_op jit(solution)/shard_map/wvg,vgq->wgq/dot_general | solution.py:133
  105.3 2.4 copy.23
  107.7 13.3 %fusion.219 = f32[32,128,16]{0,2,1:T(8,128)S(1)} fusion(f32[128,16,32]{2,1,0:T(8,128)} %fusion.39, f32[32,128,16]{0,2,1:T(8,128)} %copy.23, s32[128]{0:T(128)} %and_select_fusion.10, s32[32,32]{1,0:T(8,128)} %get-tuple-element.68), kind=kOutput, calls=%fused_computation.194 | convolution fusion | flops 26673152 | bytes 791040 | tf_op jit(solution)/shard_map/wvg,vgq->wgq/dot_general | solution.py:133
  123.9 14.7 %fusion.52 = f32[128,16,32]{2,1,0:T(8,128)} fusion(f32[32,128,16]{0,2,1:T(8,128)S(1)} %fusion.219, s32[128]{0:T(128)} %and_select_fusion.8, s32[32,32]{1,0:T(8,128)} %copy-done.3, f32[32,32]{1,0:T(8,128)} %fusion.364), kind=kOutput, calls=%fused_computation.63 | convolution fusion | flops 26607616 | bytes 532992 | tf_op jit(solution)/shard_map/wvg,vgq->wgq/dot_general | solution.py:133
  138.6 2.4 copy.25
  141.0 13.3 %fusion.213 = f32[32,128,16]{0,2,1:T(8,128)S(1)} fusion(f32[128,16,32]{2,1,0:T(8,128)} %fusion.52, f32[32,128,16]{0,2,1:T(8,128)} %copy.25, s32[128]{0:T(128)} %and_select_fusion.8, s32[32,32]{1,0:T(8,128)} %get-tuple-element.68), kind=kOutput, calls=%fused_computation.192 | convolution fusion | flops 26673152 | bytes 791040 | tf_op jit(solution)/shard_map/wvg,vgq->wgq/dot_general | solution.py:133
  155.5 3.1 collective-permute-start.4
  158.6 14.7 %fusion.65 = f32[128,16,32]{2,1,0:T(8,128)} fusion(f32[32,128,16]{0,2,1:T(8,128)S(1)} %fusion.213, s32[128]{0:T(128)} %and_select_fusion.6, s32[32,32]{1,0:T(8,128)} %copy-done.3, f32[32,32]{1,0:T(8,128)} %fusion.364), kind=kOutput, calls=%fused_computation.74 | convolution fusion | flops 26607616 | bytes 532992 | tf_op jit(solution)/shard_map/wvg,vgq->wgq/dot_general | solution.py:133
  173.3 2.4 copy.27
  175.7 13.3 %fusion.207 = f32[32,128,16]{0,2,1:T(8,128)S(1)} fusion(f32[128,16,32]{2,1,0:T(8,128)} %fusion.65, f32[32,128,16]{0,2,1:T(8,128)} %copy.27, s32[128]{0:T(128)} %and_select_fusion.6, s32[32,32]{1,0:T(8,128)} %get-tuple-element.68), kind=kOutput, calls=%fused_computation.190 | convolution fusion | flops 26673152 | bytes 791040 | tf_op jit(solution)/shard_map/wvg,vgq->wgq/dot_general | solution.py:133
  190.2 4.2 collective-permute-start.5
  194.5 14.7 %fusion.78 = f32[128,16,32]{2,1,0:T(8,128)} fusion(f32[32,128,16]{0,2,1:T(8,128)S(1)} %fusion.207, s32[128]{0:T(128)} %and_select_fusion.4, s32[32,32]{1,0:T(8,128)} %copy-done.3, f32[32,32]{1,0:T(8,128)} %fusion.364), kind=kOutput, calls=%fused_computation.85 | convolution fusion | flops 26607616 | bytes 532992 | tf_op jit(solution)/shard_map/wvg,vgq->wgq/dot_general | solution.py:133
  209.1 2.4 copy.29
  211.5 13.3 %fusion.201 = f32[32,128,16]{0,2,1:T(8,128)S(1)} fusion(f32[128,16,32]{2,1,0:T(8,128)} %fusion.78, f32[32,128,16]{0,2,1:T(8,128)} %copy.29, s32[128]{0:T(128)} %and_select_fusion.4, s32[32,32]{1,0:T(8,128)} %get-tuple-element.68), kind=kOutput, calls=%fused_computation.188 | convolution fusion | flops 26673152 | bytes 791040 | tf_op jit(solution)/shard_map/wvg,vgq->wgq/dot_general | solution.py:133
  227.5 14.7 %fusion.91 = f32[128,16,32]{2,1,0:T(8,128)} fusion(f32[32,128,16]{0,2,1:T(8,128)S(1)} %fusion.201, s32[128]{0:T(128)} %and_select_fusion.2, s32[32,32]{1,0:T(8,128)} %copy-done.3, f32[32,32]{1,0:T(8,128)} %fusion.364), kind=kOutput, calls=%fused_computation.96 | convolution fusion | flops 26607616 | bytes 532992 | tf_op jit(solution)/shard_map/wvg,vgq->wgq/dot_general | solution.py:133
  242.2 2.4 copy.31
  244.6 13.3 %fusion.195 = f32[32,128,16]{0,2,1:T(8,128)S(1)} fusion(f32[128,16,32]{2,1,0:T(8,128)} %fusion.91, f32[32,128,16]{0,2,1:T(8,128)} %copy.31, s32[128]{0:T(128)} %and_select_fusion.2, s32[32,32]{1,0:T(8,128)} %get-tuple-element.68), kind=kOutput, calls=%fused_computation.186 | convolution fusion | flops 26673152 | bytes 791040 | tf_op jit(solution)/shard_map/wvg,vgq->wgq/dot_general | solution.py:133
  259.1 2.6 collective-permute-start.7
  261.8 14.7 %fusion.104 = f32[128,16,32]{2,1,0:T(8,128)} fusion(f32[32,128,16]{0,2,1:T(8,128)S(1)} %fusion.195, s32[128]{0:T(128)} %and_select_fusion, s32[32,32]{1,0:T(8,128)} %copy-done.3, f32[32,32]{1,0:T(8,128)} %fusion.364), kind=kOutput, calls=%fused_computation.107 | convolution fusion | flops 26607616 | bytes 532992 | tf_op jit(solution)/shard_map/wvg,vgq->wgq/dot_general | solution.py:133
  277.9 14.2 %fusion.189 = f32[32,128,16]{0,2,1:T(8,128)S(1)} fusion(f32[128,16,32]{2,1,0:T(8,128)} %fusion.104, f32[32,128,16]{0,2,1:T(8,128)S(1)} %copy.33, s32[128]{0:T(128)} %and_select_fusion, s32[32,32]{1,0:T(8,128)} %get-tuple-element.68), kind=kOutput, calls=%fused_computation.184 | convolution fusion | flops 26673152 | bytes 791040 | tf_op jit(solution)/shard_map/wvg,vgq->wgq/dot_general | solution.py:133
  295.3 72.4 %all-reduce = (f32[16]{0:T(128)S(1)}, f32[16]{0:T(128)S(1)}) all-reduce(f32[16]{0:T(128)S(1)} %get-tuple-element.49, f32[16]{0:T(128)S(1)} %get-tuple-element.48), channel_id=1, replica_groups=mesh['box'=256] {'box'}, use_global_device_ids=true, to_apply=%region_3.4 | all-reduce | flops 32 | bytes 256 | tf_op jit(solution)/shard_map/psum | solution.py:27
  367.9 74.4 %psum.23 = f32[16]{0:T(128)S(1)} all-reduce(f32[16]{0:T(128)S(1)} %multiply_reduce_fusion), channel_id=1, replica_groups=mesh['box'=256] {'box'}, use_global_device_ids=true, to_apply=%region_5.6 | all-reduce | flops 16 | bytes 128 | tf_op jit(solution)/shard_map/psum | solution.py:27
  443.2 12.0 %while.11 = (s32[]{:T(128)}, f32[16,2048]{1,0:T(8,128)S(1)}, f32[8,16,512]{2,1,0:T(8,128)S(1)}, s32[8,512]{1,0:T(8,128)S(1)}, s32[]{:T(128)}, /*index=5*/s32[]{:T(128)}) while((s32[]{:T(128)}, f32[16,2048]{1,0:T(8,128)S(1)}, f32[8,16,512]{2,1,0:T(8,128)S(1)}, s32[8,512]{1,0:T(8,128)S(1)}, s32[]{:T(128)}, /*index=5*/s32[]{:T(128)}) %tuple.37), condition=%wide.region_7.8_spmd.clone, body=%wide.region_6.7_spmd.clone.sunk | while | flops 202440704 | bytes 301151 | solution.py:188
  455.8 27.5 %shard_map.85 = f32[256,128]{1,0:T(8,128)} custom-call(f32[256,128]{1,0:T(8,128)} %reshape.333.x_ref), custom_call_target="tpu_custom_call" | custom-call | tf_op jit(solution)/shard_map/pallas_call | solution.py:100
  (83 shorter events, 49.4 us)
Async XLA Ops:
  2.5 3.3 copy-start
  13.4 26.4 %collective-permute-start = (f32[32,128,16]{1,2,0:T(8,128)}, f32[32,128,16]{1,2,0:T(8,128)}, u32[]{:S(2)}, u32[]{:S(2)}) collective-permute-start(f32[32,128,16]{1,2,0:T(8,128)} %copy.18), channel_id=1, source_target_pairs={{0,1},{1,0},{2,3},{3,2},{4,5},{5,4},{6,7},{7,6},{8,9},{9,8},{10,11... | collective-permute-start | bytes 786440 | tf_op jit(solution)/shard_map/ppermute | solution.py:23
  25.1 14.7 %copy-start.3 = (s32[32,32]{1,0:T(8,128)}, s32[32,32]{1,0:T(8,128)S(1)}, u32[]{:S(2)}) copy-start(s32[32,32]{1,0:T(8,128)S(1)} %get-tuple-element.69) | copy-start | bytes 12292
  56.7 14.7 %collective-permute-start.1 = (f32[32,128,16]{1,2,0:T(8,128)}, f32[32,128,16]{1,2,0:T(8,128)}, u32[]{:S(2)}, u32[]{:S(2)}) collective-permute-start(f32[32,128,16]{1,2,0:T(8,128)} %copy.20), channel_id=1, source_target_pairs={{0,2},{1,3},{2,0},{3,1},{4,6},{5,7},{6,4},{7,5},{8,10},{9,11},{10,... | collective-permute-start | bytes 786440 | tf_op jit(solution)/shard_map/ppermute | solution.py:23
  88.3 17.0 %collective-permute-start.2 = (f32[32,128,16]{1,2,0:T(8,128)}, f32[32,128,16]{1,2,0:T(8,128)}, u32[]{:S(2)}, u32[]{:S(2)}) collective-permute-start(f32[32,128,16]{1,2,0:T(8,128)} %copy.22), channel_id=1, source_target_pairs={{0,4},{1,5},{2,6},{3,7},{4,0},{5,1},{6,2},{7,3},{8,12},{9,13},{10,... | collective-permute-start | bytes 786440 | tf_op jit(solution)/shard_map/ppermute | solution.py:23
  122.3 16.3 %collective-permute-start.3 = (f32[32,128,16]{1,2,0:T(8,128)}, f32[32,128,16]{1,2,0:T(8,128)}, u32[]{:S(2)}, u32[]{:S(2)}) collective-permute-start(f32[32,128,16]{1,2,0:T(8,128)} %copy.24), channel_id=1, source_target_pairs={{0,8},{1,9},{2,10},{3,11},{4,12},{5,13},{6,14},{7,15},{8,0},{9,1},... | collective-permute-start | bytes 786440 | tf_op jit(solution)/shard_map/ppermute | solution.py:23
  155.5 17.8 %collective-permute-start.4 = (f32[32,128,16]{1,2,0:T(8,128)}, f32[32,128,16]{1,2,0:T(8,128)}, u32[]{:S(2)}, u32[]{:S(2)}) collective-permute-start(f32[32,128,16]{1,2,0:T(8,128)} %copy.26), channel_id=1, source_target_pairs={{0,16},{1,17},{2,18},{3,19},{4,20},{5,21},{6,22},{7,23},{8,24},{9,... | collective-permute-start | bytes 786440 | tf_op jit(solution)/shard_map/ppermute | solution.py:23
  190.2 18.9 %collective-permute-start.5 = (f32[32,128,16]{1,2,0:T(8,128)}, f32[32,128,16]{1,2,0:T(8,128)}, u32[]{:S(2)}, u32[]{:S(2)}) collective-permute-start(f32[32,128,16]{1,2,0:T(8,128)} %copy.28), channel_id=1, source_target_pairs={{0,32},{1,33},{2,34},{3,35},{4,36},{5,37},{6,38},{7,39},{8,40},{9,... | collective-permute-start | bytes 786440 | tf_op jit(solution)/shard_map/ppermute | solution.py:23
  226.1 16.2 %collective-permute-start.6 = (f32[32,128,16]{1,2,0:T(8,128)}, f32[32,128,16]{1,2,0:T(8,128)}, u32[]{:S(2)}, u32[]{:S(2)}) collective-permute-start(f32[32,128,16]{1,2,0:T(8,128)} %copy.30), channel_id=1, source_target_pairs={{0,64},{1,65},{2,66},{3,67},{4,68},{5,69},{6,70},{7,71},{8,72},{9,... | collective-permute-start | bytes 786440 | tf_op jit(solution)/shard_map/ppermute | solution.py:23
  259.1 17.3 %collective-permute-start.7 = (f32[32,128,16]{1,2,0:T(8,128)}, f32[32,128,16]{1,2,0:T(8,128)}, u32[]{:S(2)}, u32[]{:S(2)}) collective-permute-start(f32[32,128,16]{1,2,0:T(8,128)} %copy.32), channel_id=1, source_target_pairs={{0,128},{1,129},{2,130},{3,131},{4,132},{5,133},{6,134},{7,135},{8... | collective-permute-start | bytes 786440 | tf_op jit(solution)/shard_map/ppermute | solution.py:23
  294.2 0.9 copy-start.1
  294.2 73.7 %copy-start.2 = (s32[4096]{0:T(1024)S(1)}, s32[4096]{0:T(1024)}, u32[]{:S(2)}) copy-start(s32[4096]{0:T(1024)} %param.12) | copy-start | bytes 49156

commit v2 on v0

v2 whole, which is shorter than its diff:
```python
import functools
import math

import jax
import jax.numpy as jnp
from jax import lax
from jax.experimental import pallas as pl
from jax.experimental.pallas import tpu as pltpu
from jax.sharding import PartitionSpec as P

AXIS = "box"
DEVICES = 256
CHIPS = 128
CORES = 2
WIDTH = 32
RANK = 16
LEAF = 32
COLUMNS = 16
SKETCH = 2048
SECTIONS = 8
BOXES = 128
LANES = 128
POINTS = BOXES * LEAF
CHUNKS = POINTS // LANES
TOTAL = POINTS * DEVICES
MODULUS = 8191
EPSILON = 1e-06
SLOT = 8
SENT = 6
BACK = 5
LOW = 256
HIGH = SKETCH // LOW
PIECES = 3
STATE = COLUMNS * WIDTH
MESH = pl.DeviceIdType.MESH

SINE = (3.141592580044348, -5.1677068789061815, 2.550031376988974, -0.5980451725653999, 0.07722012618330765)
COSINE = (
    0.9999999997799037,
    -4.9348021370788295,
    4.058709159556463,
    -1.3352120030521555,
    0.23493731382438812,
    -0.024396324364030414,
)


def fold(x):
    x = (x & MODULUS) + (x >> 13)
    return (x & MODULUS) + (x >> 13)


def turns(phase):
    return (phase << 19) + (phase << 6) + (phase >> 7)


def poly(coefs, y):
    total = jnp.float32(coefs[-1])
    for coef in coefs[-2::-1]:
        total = total * y + jnp.float32(coef)
    return total


def cosine(turn, amplitude):
    r = turn.astype(jnp.float32) * jnp.float32(2.0**-32)
    s = r * poly(SINE, r * r)
    return amplitude - (2.0 * amplitude) * (s * s)


def both(turn, amplitude):
    r = turn.astype(jnp.float32) * jnp.float32(2.0**-32)
    y = r * r
    s = r * poly(SINE, y)
    c = poly(COSINE, y)
    return amplitude - (2.0 * amplitude) * (s * s), (2.0 * amplitude) * (s * c)


def swap_groups(parts):
    parts = list(parts)
    lane = lax.broadcasted_iota(jnp.int32, parts[0].shape, 1)
    for bit in (1, 2):
        shift = 32 * bit
        low = (lane & shift) == 0
        for i in range(4):
            if i & bit:
                continue
            a, b = parts[i], parts[i | bit]
            parts[i] = jnp.where(low, a, pltpu.roll(b, shift, 1))
            parts[i | bit] = jnp.where(low, pltpu.roll(a, LANES - shift, 1), b)
    return parts


def to_lanes(column, offset):
    rows = column.shape[0]
    shape = (rows, LANES)
    here = lax.broadcasted_iota(jnp.int32, shape, 1) == lax.broadcasted_iota(jnp.int32, shape, 0) + offset
    return jnp.sum(jnp.where(here, jnp.broadcast_to(column, shape), 0.0), axis=0, keepdims=True)


def to_column(row, offset, rows):
    shape = (rows, LANES)
    here = lax.broadcasted_iota(jnp.int32, shape, 1) == lax.broadcasted_iota(jnp.int32, shape, 0) + offset
    return jnp.sum(jnp.where(here, jnp.broadcast_to(row, shape), 0.0), axis=1, keepdims=True)


def combine(out_ref, terms, add=False):
    group = 4

    def one_group(g, carry):
        first = pl.multiple_of(g * group * WIDTH, group * WIDTH)
        if add:
            acc = [out_ref[pl.ds(first + 8 * i, 8), :] for i in range(4 * group)]
        else:
            acc = [jnp.zeros((8, LANES), jnp.float32) for _ in range(4 * group)]

        def step(v, acc):
            acc = list(acc)
            for m_ref, base, c_ref in terms:
                rows = [m_ref[pl.ds(pl.multiple_of(base + v * WIDTH, WIDTH) + 8 * t, 8), :] for t in range(4)]
                for i in range(group):
                    c = c_ref[pl.ds(first + i * WIDTH + v, 8, stride=0), :]
                    for t in range(4):
                        acc[4 * i + t] = acc[4 * i + t] + rows[t] * c
            return tuple(acc)

        acc = lax.fori_loop(0, WIDTH, step, tuple(acc), unroll=4)
        for i in range(4 * group):
            out_ref[pl.ds(first + 8 * i, 8), :] = acc[i]
        return carry

    lax.fori_loop(0, COLUMNS // group, one_group, 0)


def build_onehot(onehot_ref, rows_ref):
    def one(c, carry):
        low = jnp.broadcast_to(rows_ref[pl.ds(c, 1), :] & (LOW - 1), (LOW, LANES))
        hit = low == lax.broadcasted_iota(jnp.int32, (LOW, LANES), 0)
        onehot_ref[:, pl.ds(pl.multiple_of(c * LANES, LANES), LANES)] = jnp.where(hit, 1.0, 0.0).astype(jnp.bfloat16)
        return carry

    lax.fori_loop(0, CHUNKS, one, 0, unroll=2)


def scatter_sum(sums_ref, left_ref, onehot_ref, rows_ref, signs_ref, values, acc_ref):
    def one(c, carry):
        x = values(c) * jnp.broadcast_to(signs_ref[pl.ds(c, 1), :], (COLUMNS, LANES))
        high = jnp.broadcast_to(rows_ref[pl.ds(c, 1), :] >> 8, (COLUMNS, LANES))
        here = pl.ds(pl.multiple_of(c * LANES, LANES), LANES)
        pieces = []
        for _ in range(PIECES):
            piece = x.astype(jnp.bfloat16)
            x = x - piece.astype(jnp.float32)
            pieces.append(piece)
        for h in range(HIGH):
            mask = jnp.where(high == h, 1.0, 0.0).astype(jnp.bfloat16)
            for i, piece in enumerate(pieces):
                left_ref[pl.ds((i * HIGH + h) * COLUMNS, COLUMNS), here] = piece * mask
        return carry

    lax.fori_loop(0, CHUNKS, one, 0, unroll=2)
    depth = 512

    def product(k):
        at = pl.ds(pl.multiple_of(k * depth, depth), depth)
        return lax.dot_general(
            left_ref[:, at], onehot_ref[:, at], (((1,), (1,)), ((), ())), preferred_element_type=jnp.float32
        )

    acc_ref[...] = product(0)

    def more(k, carry):
        acc_ref[...] += product(k)
        return carry

    lax.fori_loop(1, POINTS // depth, more, 0)
    rows = HIGH * COLUMNS
    total = acc_ref[pl.ds(0, rows), :] + acc_ref[pl.ds(rows, rows), :] + acc_ref[pl.ds(2 * rows, rows), :]
    for h in range(HIGH):
        for half in range(LOW // LANES):
            block = total[h * COLUMNS : (h + 1) * COLUMNS, half * LANES : (half + 1) * LANES]
            sums_ref[pl.ds(h * (LOW // LANES) + half, COLUMNS, stride=SKETCH // LANES), :] = block


def make_sections(matrix_ref, scale, group, chip):
    own_size = 0.35 / math.sqrt(WIDTH)
    cross_size = 0.6 / math.sqrt(WIDTH)
    sub = lax.broadcasted_iota(jnp.int32, (8, LANES), 0)
    box = group * BOXES + chip

    def one(k, carry):
        key = box * 37 + 101 * k
        guess = (key.astype(jnp.float32) * jnp.float32(1.0 / (MODULUS - 1))).astype(jnp.int32)
        key = key - guess * (MODULUS - 1)
        key = jnp.where(key < 0, key + (MODULUS - 1), key)
        key = jnp.where(key >= MODULUS - 1, key - (MODULUS - 1), key)
        unit = fold(scale * (key + 1))
        base = pl.multiple_of(k * (2 * WIDTH * WIDTH), 2 * WIDTH * WIDTH)
        half = turns(jnp.int32(4096))
        for t in range(4):
            own_step = turns(fold((sub + (8 * t + 1)) * unit))
            cross_step = turns(fold((sub + (8 * t + 3)) * unit))
            own_turn = own_step
            cross_turn = jnp.broadcast_to(half, (8, LANES))
            for v in range(WIDTH):
                own_turn = own_turn + own_step
                cross_turn = cross_turn + cross_step
                own = cosine(own_turn, own_size)
                if v // 8 == t:
                    own = own + jnp.where(sub == v % 8, 0.85, 0.0)
                matrix_ref[pl.ds(base + v * WIDTH + 8 * t, 8), :] = own
                matrix_ref[pl.ds(base + WIDTH * WIDTH + v * WIDTH + 8 * t, 8), :] = cosine(cross_turn, cross_size)
        return carry

    return one


def kernel(
    basis_ref, diag_ref, coords_ref, scale_ref, rows_ref, signs_ref,
    new_ref, sketch_ref, arnoldi_ref,
    tall, pack, flat_x, out_box, in_box, matrix, leaf, leaf_t, state_x,
    first, second, first_p, partner, point, point_rows, residual,
    out_back, in_back, onehot, left, acc, sums_b, parts_b, row_b, all_b, sums_r, parts_r, row_r, all_r,
    half_mine, half_other, shift_rows, signs_f,
    fwd_s, fwd_r, ex_s, ex_r, rsb_s, rsb_r, agb_s, agb_r, rs_s, rs_r, ag_s, ag_r, back_s, back_r, mom_s, mom_r,
):
    me = lax.axis_index(AXIS)
    chip = me // CORES
    core = lax.rem(me, CORES)
    other = me + 1 - 2 * core
    barrier = pltpu.get_barrier_semaphore()
    peers = DEVICES - 1
    mates = CHIPS - 1

    def peer(step):
        return lax.rem(me + step + 1, DEVICES)

    def mate(step):
        return lax.rem(me + CORES * (step + 1), DEVICES)

    def each(count, what, unroll=1):
        def body(step, carry):
            what(step)
            return carry

        lax.fori_loop(0, count, body, 0, unroll=unroll)

    def remote(src, dst, send, recv, to):
        return pltpu.make_async_remote_copy(
            src_ref=src, dst_ref=dst, send_sem=send, recv_sem=recv, device_id=(to,), device_id_type=MESH
        )

    def settle(ref, rows, sem):
        pltpu.make_async_copy(ref.at[pl.ds(0, rows)], ref.at[pl.ds(0, rows)], sem).wait()

    each(peers, lambda i: pl.semaphore_signal(barrier, inc=1, device_id=(peer(i),), device_id_type=MESH))

    square = jnp.zeros((COLUMNS, LANES), jnp.float32)
    weighted = jnp.zeros((COLUMNS, LANES), jnp.float32)
    for c in range(CHUNKS):
        x = basis_ref[:, c * LANES : (c + 1) * LANES]
        tall[pl.ds(c * COLUMNS, COLUMNS), :] = x
        pack[pl.ds(2 * c, 2), :] = coords_ref[:, c * LANES : (c + 1) * LANES].astype(jnp.float32)
        d = jnp.broadcast_to(diag_ref[pl.ds(c, 1), :], (COLUMNS, LANES))
        square = square + x * x
        weighted = weighted + d * x * x
    moments = to_lanes(jnp.sum(square, axis=1, keepdims=True), 32) + to_lanes(
        jnp.sum(weighted, axis=1, keepdims=True), 48
    )
    sign = (2 * signs_ref[...] - 1).astype(jnp.float32)
    signs_f[...] = sign
    for rho in range(4):
        blocks = swap_groups([tall[pl.ds(4 * rho + t, CHUNKS, stride=COLUMNS), :] for t in range(4)])
        for j in range(4):
            out_box[pl.ds(SLOT * j + rho, CHUNKS, stride=4 * SLOT), :] = blocks[j]
    blocks = swap_groups(
        [
            pack[pl.ds(0, CHUNKS, stride=2), :],
            pack[pl.ds(1, CHUNKS, stride=2), :],
            diag_ref[...],
            rows_ref[...].astype(jnp.float32),
        ]
    )
    for j in range(4):
        out_box[pl.ds(SLOT * j + 4, CHUNKS, stride=4 * SLOT), :] = blocks[j]
    zero = jnp.zeros((CHUNKS, LANES), jnp.float32)
    blocks = swap_groups([sign, zero, zero, zero])
    for j in range(4):
        out_box[pl.ds(SLOT * j + 5, CHUNKS, stride=4 * SLOT), :] = blocks[j] + moments

    scale = lax.rem(scale_ref[0], MODULUS)
    group = lax.broadcasted_iota(jnp.int32, (8, LANES), 1) * CORES + core
    section = make_sections(matrix, scale, group, chip)
    lax.fori_loop(0, 4, section, 0)

    pl.semaphore_wait(barrier, peers)

    def send_box(i):
        to = mate(i)
        remote(
            out_box.at[pl.ds(pl.multiple_of(SLOT * (to // CORES), SLOT), SENT)],
            in_box.at[pl.ds(pl.multiple_of(SLOT * chip, SLOT), SENT)],
            fwd_s, fwd_r, to,
        ).start()

    each(mates, send_box)
    mine = pl.ds(pl.multiple_of(SLOT * chip, SLOT), SLOT)
    in_box[mine, :] = out_box[mine, :]
    lax.fori_loop(4, SECTIONS, section, 0)

    build_onehot(onehot, rows_ref)
    scatter_sum(
        sums_b, left, onehot, rows_ref, signs_f,
        lambda c: tall[pl.ds(pl.multiple_of(c * COLUMNS, COLUMNS), COLUMNS), :], acc,
    )

    def spread_rows(src, dst, send, recv):
        def go(i):
            to = peer(i)
            remote(src.at[pl.ds(to, 1)], dst.at[pl.ds(me, 1)], send, recv, to).start()

        each(peers, go)
        dst[pl.ds(me, 1), :] = src[pl.ds(me, 1), :]

    def gather_rows(row, dst, send, recv):
        def go(i):
            remote(row, dst.at[pl.ds(me, 1)], send, recv, peer(i)).start()

        each(peers, go)
        dst[pl.ds(me, 1), :] = row[...]

    spread_rows(sums_b, parts_b, rsb_s, rsb_r)

    settle(in_box, mates * SENT, fwd_r)
    for rho in range(4):
        state_x[pl.ds(rho * LANES, LANES), :] = in_box[pl.ds(rho, CHIPS, stride=SLOT), :].T
    point[...] = in_box[pl.ds(4, CHIPS, stride=SLOT), :].T
    tail = in_box[pl.ds(5, CHIPS, stride=SLOT), :].T
    signs_f[...] = tail[0:LEAF, :]
    point_rows[...] = point[pl.ds(3 * LEAF, LEAF), :].astype(jnp.int32)
    first[pl.ds(STATE, 2 * COLUMNS), :] = jnp.broadcast_to(
        jnp.sum(tail[LEAF : LEAF + 2 * COLUMNS, :], axis=1, keepdims=True), (2 * COLUMNS, LANES)
    )

    size = 1.0 / math.sqrt(LEAF)
    across = point[pl.ds(0, LEAF), :].astype(jnp.int32) * scale
    down = point[pl.ds(LEAF, LEAF), :].astype(jnp.int32) * scale
    turn_x = [turns(fold(across * f)) for f in range(1, 5)]
    turn_y = [turns(fold(down * f)) for f in range(1, 5)]
    for w in range(RANK):
        c, s = both(turn_x[w % 4] + turn_y[w // 4], size)
        for at, table in ((w, c), (w + RANK, s)):
            leaf[pl.ds(at * LEAF, LEAF), :] = table
            leaf_t[pl.ds(at, LEAF, stride=WIDTH), :] = table
    combine(first, [(leaf_t, 0, state_x)])

    exchange = remote(first, first_p, ex_s, ex_r, other)
    exchange.start()
    combine(second, [(matrix, 0, first)])
    build_onehot(onehot, point_rows)
    exchange.wait_recv()
    combine(second, [(matrix, WIDTH * WIDTH, first_p)], add=True)
    exchange.wait_send()

    source, target = second, first
    for k in range(1, SECTIONS):
        step = 1 << (k - 1)

        def swap(r, source=source, step=step):
            at = pl.ds(pl.multiple_of(r * 64, 64), 64)
            a = source[at, :]
            up = (lax.broadcasted_iota(jnp.int32, a.shape, 1) & step) != 0
            partner[at, :] = jnp.where(up, pltpu.roll(a, step, 1), pltpu.roll(a, LANES - step, 1))

        each(STATE // 64, swap)
        base = k * 2 * WIDTH * WIDTH
        combine(target, [(matrix, base, source), (matrix, base + WIDTH * WIDTH, partner)])
        source, target = target, source
        if k == 2:
            settle(parts_b, peers, rsb_r)
            row_b[...] = jnp.sum(parts_b[...], axis=0, keepdims=True)
            gather_rows(row_b, all_b, agb_s, agb_r)

    both_sums = first_p[pl.ds(STATE, 2 * COLUMNS), :] + half_mine_sum(first)
    total_b = both_sums[0:COLUMNS, :]
    total_db = both_sums[COLUMNS:, :]
    weight = total_b + EPSILON * TOTAL
    shift_rows[...] = total_db / weight
    combine(residual, [(leaf, 0, source)])
    cross_sum = []
    square_sum = []
    for q in range(COLUMNS):
        p0 = jnp.broadcast_to(shift_rows[pl.ds(q, 1), :], (LEAF, LANES))
        b = state_x[pl.ds(q * LEAF, LEAF), :]
        r = (point[pl.ds(2 * LEAF, LEAF), :] - p0) * b + residual[pl.ds(q * LEAF, LEAF), :]
        residual[pl.ds(q * LEAF, LEAF), :] = r
        cross_sum.append(jnp.sum(b * r, axis=0, keepdims=True))
        square_sum.append(jnp.sum(r * r, axis=0, keepdims=True))
    moments = jnp.sum(jnp.concatenate(cross_sum + square_sum, axis=0), axis=1, keepdims=True)
    scatter_sum(
        sums_r, left, onehot, point_rows, signs_f,
        lambda c: residual[pl.ds(c, COLUMNS, stride=LEAF), :], acc,
    )
    spread_rows(sums_r, parts_r, rs_s, rs_r)

    for rho in range(4):
        out_back[pl.ds(rho, CHIPS, stride=SLOT), :] = residual[pl.ds(rho * LANES, LANES), :].T
    out_back[pl.ds(4, CHIPS, stride=SLOT), :] = jnp.broadcast_to(to_lanes(moments, 0), (CHIPS, LANES))

    def send_back(i):
        to = mate(i)
        remote(
            out_back.at[pl.ds(pl.multiple_of(SLOT * (to // CORES), SLOT), BACK)],
            in_back.at[pl.ds(pl.multiple_of(SLOT * chip, SLOT), BACK)],
            back_s, back_r, to,
        ).start()

    each(mates, send_back)
    in_back[mine, :] = out_back[mine, :]

    settle(parts_r, peers, rs_r)
    row_r[...] = jnp.sum(parts_r[...], axis=0, keepdims=True)
    gather_rows(row_r, all_r, ag_s, ag_r)

    settle(in_back, mates * BACK, back_r)
    half_mine[...] = jnp.broadcast_to(
        jnp.sum(in_back[pl.ds(4, CHIPS, stride=SLOT), :], axis=0, keepdims=True), (8, LANES)
    )
    swap_sums = remote(half_mine, half_other, mom_s, mom_r, other)
    swap_sums.start()
    for rho in range(4):
        blocks = swap_groups([in_back[pl.ds(SLOT * j + rho, CHUNKS, stride=4 * SLOT), :] for j in range(4)])
        for t in range(4):
            flat_x[pl.ds(4 * rho + t, CHUNKS, stride=COLUMNS), :] = blocks[t]
    swap_sums.wait()
    sums = to_column(half_mine[0:1, :] + half_other[0:1, :], 0, 2 * COLUMNS)
    sums = jnp.broadcast_to(sums, (2 * COLUMNS, LANES))
    m1 = sums[0:COLUMNS, :]
    m2 = sums[COLUMNS:, :]
    p0 = shift_rows[...]
    delta = (m1 - p0 * (EPSILON * TOTAL)) / weight
    energy = m2 - 2.0 * delta * m1 + delta * delta * total_b
    spread = jnp.sqrt(jnp.maximum(energy, 0.0) * (1.0 / TOTAL) + EPSILON)
    inverse = 1.0 / spread
    arnoldi_ref[0:1, :] = to_lanes((p0 + delta)[:, 0:1], 0)[:, 0:COLUMNS]
    arnoldi_ref[1:2, :] = to_lanes(spread[:, 0:1], 0)[:, 0:COLUMNS]
    for c in range(CHUNKS):
        at = pl.ds(c * COLUMNS, COLUMNS)
        new_ref[:, c * LANES : (c + 1) * LANES] = (flat_x[at, :] - delta * tall[at, :]) * inverse

    settle(all_b, peers, agb_r)
    settle(all_r, peers, ag_r)
    factor = inverse * math.sqrt(SKETCH / TOTAL)
    for r in range(SKETCH // LANES):
        at = pl.ds(r, COLUMNS, stride=SKETCH // LANES)
        sketch_ref[:, r * LANES : (r + 1) * LANES] = (all_r[at, :] - delta * all_b[at, :]) * factor

    settle(out_box, mates * SENT, fwd_s)
    settle(sums_b, peers, rsb_s)
    settle(all_b, peers, agb_s)
    settle(sums_r, peers, rs_s)
    settle(all_r, peers, ag_s)
    settle(out_back, mates * BACK, back_s)


def half_mine_sum(first):
    return first[pl.ds(STATE, 2 * COLUMNS), :]


def body(basis_vector, diagonal, coords, phase_scale, sketch_rows, sketch_signs):
    f32 = jnp.float32
    vmem = pl.BlockSpec(memory_space=pltpu.VMEM)
    box_rows = CHIPS * SLOT
    scratch = [
        pltpu.VMEM((CHUNKS * COLUMNS, LANES), f32),
        pltpu.VMEM((2 * CHUNKS, LANES), f32),
        pltpu.VMEM((CHUNKS * COLUMNS, LANES), f32),
        pltpu.VMEM((box_rows, LANES), f32),
        pltpu.VMEM((box_rows, LANES), f32),
        pltpu.VMEM((SECTIONS * 2 * WIDTH * WIDTH, LANES), f32),
        pltpu.VMEM((WIDTH * LEAF, LANES), f32),
        pltpu.VMEM((WIDTH * LEAF, LANES), f32),
        pltpu.VMEM((STATE, LANES), f32),
        pltpu.VMEM((STATE + 2 * COLUMNS, LANES), f32),
        pltpu.VMEM((STATE, LANES), f32),
        pltpu.VMEM((STATE + 2 * COLUMNS, LANES), f32),
        pltpu.VMEM((STATE, LANES), f32),
        pltpu.VMEM((4 * LEAF, LANES), f32),
        pltpu.VMEM((LEAF, LANES), jnp.int32),
        pltpu.VMEM((STATE, LANES), f32),
        pltpu.VMEM((box_rows, LANES), f32),
        pltpu.VMEM((box_rows, LANES), f32),
        pltpu.VMEM((LOW, POINTS), jnp.bfloat16),
        pltpu.VMEM((PIECES * HIGH * COLUMNS, POINTS), jnp.bfloat16),
        pltpu.VMEM((PIECES * HIGH * COLUMNS, LOW), f32),
    ]
    for _ in range(2):
        scratch += [
            pltpu.VMEM((DEVICES, LANES), f32),
            pltpu.VMEM((DEVICES, LANES), f32),
            pltpu.VMEM((1, LANES), f32),
            pltpu.VMEM((DEVICES, LANES), f32),
        ]
    scratch += [
        pltpu.VMEM((8, LANES), f32),
        pltpu.VMEM((8, LANES), f32),
        pltpu.VMEM((COLUMNS, LANES), f32),
        pltpu.VMEM((LEAF, LANES), f32),
    ]
    scratch += [pltpu.SemaphoreType.DMA] * 16
    call = pl.pallas_call(
        kernel,
        out_shape=(
            jax.ShapeDtypeStruct((COLUMNS, POINTS), f32),
            jax.ShapeDtypeStruct((COLUMNS, SKETCH), f32),
            jax.ShapeDtypeStruct((2, COLUMNS), f32),
        ),
        in_specs=[vmem, vmem, vmem, pl.BlockSpec(memory_space=pltpu.SMEM), vmem, vmem],
        out_specs=(vmem, vmem, vmem),
        scratch_shapes=scratch,
        compiler_params=pltpu.CompilerParams(collective_id=1, has_side_effects=True, vmem_limit_bytes=48 << 20),
    )
    table = (CHUNKS, LANES)
    return call(
        basis_vector,
        diagonal.reshape(table),
        coords,
        phase_scale,
        sketch_rows.reshape(table),
        sketch_signs.reshape(table),
    )


def solution(mesh):
    placed = (P(None, AXIS), P(AXIS), P(None, AXIS), P(), P(AXIS), P(AXIS))
    return jax.shard_map(
        body, mesh=mesh, in_specs=placed, out_specs=(P(None, AXIS), P(), P()), check_vma=False
    )
```

time: 651 us -> 80 us (0.12); the launches traced: 642 us -> 79.6 us
  matrix products: 244 us -> 0 us
  waiting for transfers between devices: 238 us -> 0 us
  Pallas kernels: 0 us -> 72.6 us
  blocking collectives: 71.8 us -> 0 us
  local copies, waits for them, and re-layouts: 40.7 us -> 5.77 us
  starting transfers between devices: 19.1 us -> 0 us
  between operations: 15.1 us -> 1.3 us
  other arithmetic: 13.4 us -> 0 us
    dot_general x26 -> x0, matrix products: 244 us -> none  [the longest x16 225 us: mix(): jnp.einsum('wvg,vgq->wgq', matrix, coeffs, precision=lax.Precision.HIGHEST)]
    psum x1 -> x0, waiting for transfers between devices: 238 us -> none  [body(): sketch = lax.psum(total, BOX) * sketch_factor]
    pallas_call x0 -> x1, Pallas kernels: none -> 72.6 us  [body(): call(basis_vector, diagonal.reshape(table), coords, phase_scale, sketch_r...]
    psum x8 -> x0, blocking collectives: 71.8 us -> none  [one_axis_at_a_time(): return functools.reduce(lax.psum, axes, x)]
    ppermute x8 -> x0, starting transfers between devices: 19 us -> none  [swapped(): lax.ppermute(x, axis, [(i, i ^ 1 << bit) for i in range(lax.axis_size(axi...]
    ppermute x8 -> x0, local copies, waits for them, and re-layouts: 18.3 us -> none  [swapped(): lax.ppermute(x, axis, [(i, i ^ 1 << bit) for i in range(lax.axis_size(axi...]
    add x7 -> x0, local copies, waits for them, and re-layouts: 8.21 us -> none  [one_segment(): return mix(own_map, coeffs) + mix(cross_map, partner)]
  transfers between devices with their start and end apart: 9 -> 0, of which waited for: 1 -> 0; matrix products, arithmetic and copies ran while one was open for 20% -> 0% of each run, Pallas kernels for 0% -> 0%
where the time goes in v2:
time: 80 us; the launch traced here: 79.6 us
  Pallas kernels  72.6 us (91%)
  local copies, waits for them, and re-layouts  5.77 us (7%)
  between operations  1.3 us (2%)
    pallas_call x1, Pallas kernels, body(): call(basis_vector, diagonal.reshape(table), coords, phase_scale, sketch_r...  72.6 us
    unnamed x13, local copies, waits for them, and re-layouts  5.77 us

profile of v2, /device:TPU:1, one launch (start us, length us, event | category | flops | bytes accessed | tf_op | source)
XLA Modules:
  0.0 79.6 jit_solution(725685638452905846)
XLA Ops:
  1.3 0.0 copy-start
  1.3 0.9 %copy-done = f32[16,4096]{1,0:T(8,128)S(1)} copy-done((f32[16,4096]{1,0:T(8,128)S(1)}, f32[16,4096]{1,0:T(8,128)}, u32[]{:S(2)}) %copy-start) | copy-done | bytes 262168
  2.2 0.0 copy-start.1
  2.2 0.8 copy-done.1
  3.0 0.0 copy-start.2
  3.0 0.7 copy-done.2
  3.7 0.0 copy-start.3
  3.7 0.7 copy-done.3
  4.4 0.0 copy-start.4
  4.4 0.7 copy-done.4
  5.1 72.6 %shard_map.85 = (f32[16,4096]{1,0:T(8,128)S(1)}, f32[16,2048]{1,0:T(8,128)S(1)}, f32[2,16]{1,0:T(2,128)S(1)}) custom-call(f32[16,4096]{1,0:T(8,128)S(1)} %copy-done, f32[32,128]{1,0:T(8,128)S(1)} %bitcast.3, s32[2,4096]{1,0:T(2,128)S(1)} %copy-done.1, s32[1]{0:T(128)S(6)} %copy.12.scale_ref, s32[32,128]{1,0:T(8,128)S(1)} %bitcast.4, s32[32,128]{1,0:T(8,128)S(1)} %bitcast.5), custom_call_target="tpu_custom_call" | custom-call | tf_op jit(solution)/shard_map/pallas_call | solution.py:523
  77.7 0.7 copy.13
  78.4 0.7 copy.14
  79.1 0.6 copy.15
Async XLA Ops:
  1.3 1.0 %copy-start = (f32[16,4096]{1,0:T(8,128)S(1)}, f32[16,4096]{1,0:T(8,128)}, u32[]{:S(2)}) copy-start(f32[16,4096]{1,0:T(8,128)} %basis_ref.1) | copy-start | bytes 786436
  2.2 0.8 copy-start.1
  3.0 0.7 copy-start.2
  3.7 0.7 copy-start.3
  4.4 0.7 copy-start.4

commit v3 on v2

--- a/solution.py
+++ b/solution.py
@@ -30,7 +30,7 @@
 BACK = 5
 LOW = 256
 HIGH = SKETCH // LOW
-PIECES = 3
+PIECES = 2
 STATE = COLUMNS * WIDTH
 MESH = pl.DeviceIdType.MESH
 
@@ -123,7 +123,7 @@
                         acc[4 * i + t] = acc[4 * i + t] + rows[t] * c
             return tuple(acc)
 
-        acc = lax.fori_loop(0, WIDTH, step, tuple(acc), unroll=4)
+        acc = lax.fori_loop(0, WIDTH, step, tuple(acc), unroll=8)
         for i in range(4 * group):
             out_ref[pl.ds(first + 8 * i, 8), :] = acc[i]
         return carry
@@ -133,9 +133,15 @@
 
 def build_onehot(onehot_ref, rows_ref):
     def one(c, carry):
-        low = jnp.broadcast_to(rows_ref[pl.ds(c, 1), :] & (LOW - 1), (LOW, LANES))
-        hit = low == lax.broadcasted_iota(jnp.int32, (LOW, LANES), 0)
-        onehot_ref[:, pl.ds(pl.multiple_of(c * LANES, LANES), LANES)] = jnp.where(hit, 1.0, 0.0).astype(jnp.bfloat16)
+        low = (rows_ref[pl.ds(c, 1), :] & (LOW - 1)).astype(jnp.float32)
+        low = jnp.broadcast_to(low, (16, LANES)).astype(jnp.bfloat16)
+        sub = lax.broadcasted_iota(jnp.int32, (16, LANES), 0).astype(jnp.float32)
+        one_b = jnp.ones((16, LANES), jnp.bfloat16)
+        zero_b = jnp.zeros((16, LANES), jnp.bfloat16)
+        here = pl.ds(pl.multiple_of(c * LANES, LANES), LANES)
+        for r in range(LOW // 16):
+            hit = low == (sub + float(16 * r)).astype(jnp.bfloat16)
+            onehot_ref[pl.ds(16 * r, 16), here] = jnp.where(hit, one_b, zero_b)
         return carry
 
     lax.fori_loop(0, CHUNKS, one, 0, unroll=2)
@@ -144,7 +150,9 @@
 def scatter_sum(sums_ref, left_ref, onehot_ref, rows_ref, signs_ref, values, acc_ref):
     def one(c, carry):
         x = values(c) * jnp.broadcast_to(signs_ref[pl.ds(c, 1), :], (COLUMNS, LANES))
-        high = jnp.broadcast_to(rows_ref[pl.ds(c, 1), :] >> 8, (COLUMNS, LANES))
+        high = (rows_ref[pl.ds(c, 1), :] >> 8).astype(jnp.float32)
+        high = jnp.broadcast_to(high, (COLUMNS, LANES)).astype(jnp.bfloat16)
+        zero_b = jnp.zeros((COLUMNS, LANES), jnp.bfloat16)
         here = pl.ds(pl.multiple_of(c * LANES, LANES), LANES)
         pieces = []
         for _ in range(PIECES):
@@ -152,29 +160,17 @@
             x = x - piece.astype(jnp.float32)
             pieces.append(piece)
         for h in range(HIGH):
-            mask = jnp.where(high == h, 1.0, 0.0).astype(jnp.bfloat16)
+            hit = high == jnp.full((COLUMNS, LANES), h, jnp.bfloat16)
             for i, piece in enumerate(pieces):
-                left_ref[pl.ds((i * HIGH + h) * COLUMNS, COLUMNS), here] = piece * mask
+                left_ref[pl.ds((i * HIGH + h) * COLUMNS, COLUMNS), here] = jnp.where(hit, piece, zero_b)
         return carry
 
     lax.fori_loop(0, CHUNKS, one, 0, unroll=2)
-    depth = 512
-
-    def product(k):
-        at = pl.ds(pl.multiple_of(k * depth, depth), depth)
-        return lax.dot_general(
-            left_ref[:, at], onehot_ref[:, at], (((1,), (1,)), ((), ())), preferred_element_type=jnp.float32
-        )
-
-    acc_ref[...] = product(0)
-
-    def more(k, carry):
-        acc_ref[...] += product(k)
-        return carry
-
-    lax.fori_loop(1, POINTS // depth, more, 0)
+    acc_ref[...] = lax.dot_general(
+        left_ref[...], onehot_ref[...], (((1,), (1,)), ((), ())), preferred_element_type=jnp.float32
+    )
     rows = HIGH * COLUMNS
-    total = acc_ref[pl.ds(0, rows), :] + acc_ref[pl.ds(rows, rows), :] + acc_ref[pl.ds(2 * rows, rows), :]
+    total = acc_ref[pl.ds(0, rows), :] + acc_ref[pl.ds(rows, rows), :]
     for h in range(HIGH):
         for half in range(LOW // LANES):
             block = total[h * COLUMNS : (h + 1) * COLUMNS, half * LANES : (half + 1) * LANES]
@@ -215,13 +211,16 @@
 
 
 def kernel(
-    basis_ref, diag_ref, coords_ref, scale_ref, rows_ref, signs_ref,
+    basis_hbm, diag_hbm, coords_hbm, scale_ref, rows_hbm, signs_hbm,
     new_ref, sketch_ref, arnoldi_ref,
     tall, pack, flat_x, out_box, in_box, matrix, leaf, leaf_t, state_x,
     first, second, first_p, partner, point, point_rows, residual,
+    out_c, in_c, half_b, other_b,
     out_back, in_back, onehot, left, acc, sums_b, parts_b, row_b, all_b, sums_r, parts_r, row_r, all_r,
     half_mine, half_other, shift_rows, signs_f,
+    basis_ref, diag_ref, coords_ref, rows_ref, signs_ref, load_sem,
     fwd_s, fwd_r, ex_s, ex_r, rsb_s, rsb_r, agb_s, agb_r, rs_s, rs_r, ag_s, ag_r, back_s, back_r, mom_s, mom_r,
+    coef_s, coef_r, hb_s, hb_r,
 ):
     me = lax.axis_index(AXIS)
     chip = me // CORES
@@ -231,11 +230,31 @@
     peers = DEVICES - 1
     mates = CHIPS - 1
 
-    def peer(step):
-        return lax.rem(me + step + 1, DEVICES)
-
-    def mate(step):
-        return lax.rem(me + CORES * (step + 1), DEVICES)
+    x = lax.rem(chip, 4)
+    z = lax.rem(me // 8, 8)
+    y = me // 64
+    x_at = [lax.rem(x + i, 4) * 2 for i in range(4)]
+    y_at = [lax.rem(y + i, 4) * 64 for i in range(4)]
+    core_at = [core, 1 - core]
+
+    def far_first(what, cores):
+        steps = [(a, b, c) for a in range(4) for b in range(4) for c in range(cores)]
+        steps.sort(key=lambda s: -(min(s[0], 4 - s[0]) + min(s[1], 4 - s[1]) + 0.1 * s[2]))
+        near = [[y_at[a] + x_at[b] + core_at[c] for b in range(4)] for a in range(4) for c in range(cores)]
+
+        def layer(dz, own):
+            base = lax.rem(z + dz, 8) * 8
+            for a, b, c in steps:
+                if own and (a, b, c) == (0, 0, 0):
+                    continue
+                what(near[a * cores + c][b] + base)
+
+        def body(i, carry):
+            layer(4 + ((i + 1) // 2) * (1 - 2 * lax.rem(i, 2)), False)
+            return carry
+
+        lax.fori_loop(0, 7, body, 0)
+        layer(0, True)
 
     def each(count, what, unroll=1):
         def body(step, carry):
@@ -252,7 +271,15 @@
     def settle(ref, rows, sem):
         pltpu.make_async_copy(ref.at[pl.ds(0, rows)], ref.at[pl.ds(0, rows)], sem).wait()
 
-    each(peers, lambda i: pl.semaphore_signal(barrier, inc=1, device_id=(peer(i),), device_id_type=MESH))
+    loads = []
+    for i, (src, dst) in enumerate(
+        [(basis_hbm, basis_ref), (coords_hbm, coords_ref), (diag_hbm, diag_ref), (rows_hbm, rows_ref), (signs_hbm, signs_ref)]
+    ):
+        loads.append(pltpu.make_async_copy(src, dst, load_sem.at[i]))
+        loads[-1].start()
+    far_first(lambda to: pl.semaphore_signal(barrier, inc=1, device_id=(to,), device_id_type=MESH), 2)
+    for load in loads:
+        load.wait()
 
     square = jnp.zeros((COLUMNS, LANES), jnp.float32)
     weighted = jnp.zeros((COLUMNS, LANES), jnp.float32)
@@ -288,90 +315,93 @@
         out_box[pl.ds(SLOT * j + 5, CHUNKS, stride=4 * SLOT), :] = blocks[j] + moments
 
     scale = lax.rem(scale_ref[0], MODULUS)
-    group = lax.broadcasted_iota(jnp.int32, (8, LANES), 1) * CORES + core
-    section = make_sections(matrix, scale, group, chip)
-    lax.fori_loop(0, 4, section, 0)
+    size = 1.0 / math.sqrt(LEAF)
+
+    def leaf_tables(store):
+        across = point[pl.ds(0, LEAF), :].astype(jnp.int32) * scale
+        down = point[pl.ds(LEAF, LEAF), :].astype(jnp.int32) * scale
+        turn_x = [turns(fold(across * f)) for f in range(1, 5)]
+        turn_y = [turns(fold(down * f)) for f in range(1, 5)]
+        for w in range(RANK):
+            c, s = both(turn_x[w % 4] + turn_y[w // 4], size)
+            store(w, c)
+            store(w + RANK, s)
+
+    def store_by_point(w, table):
+        leaf_t[pl.ds(w, LEAF, stride=WIDTH), :] = table
+
+    def store_by_width(w, table):
+        leaf[pl.ds(w * LEAF, LEAF), :] = table
+
+    for rho in range(4):
+        state_x[pl.ds(rho * LANES, LANES), :] = out_box[pl.ds(rho, CHIPS, stride=SLOT), :].T
+    point[...] = out_box[pl.ds(4, CHIPS, stride=SLOT), :].T
+    leaf_tables(store_by_point)
+    combine(second, [(leaf_t, 0, state_x)])
+    for rho in range(4):
+        out_c[pl.ds(rho, CHIPS, stride=SLOT), :] = second[pl.ds(rho * LANES, LANES), :].T
 
     pl.semaphore_wait(barrier, peers)
 
-    def send_box(i):
-        to = mate(i)
-        remote(
-            out_box.at[pl.ds(pl.multiple_of(SLOT * (to // CORES), SLOT), SENT)],
-            in_box.at[pl.ds(pl.multiple_of(SLOT * chip, SLOT), SENT)],
-            fwd_s, fwd_r, to,
-        ).start()
-
-    each(mates, send_box)
-    mine = pl.ds(pl.multiple_of(SLOT * chip, SLOT), SLOT)
-    in_box[mine, :] = out_box[mine, :]
-    lax.fori_loop(4, SECTIONS, section, 0)
+    def send_slots(src, dst, count, send, recv):
+        def go(to):
+            remote(
+                src.at[pl.ds(pl.multiple_of(SLOT * (to // CORES), SLOT), count)],
+                dst.at[pl.ds(pl.multiple_of(SLOT * chip, SLOT), count)],
+                send, recv, to,
+            ).start()
+
+        far_first(go, 1)
+        mine = pl.ds(pl.multiple_of(SLOT * chip, SLOT), count)
+        dst[mine, :] = src[mine, :]
+
+    send_slots(out_c, in_c, 4, coef_s, coef_r)
+
+    def spread_rows(src, dst, send, recv):
+        def go(to):
+            remote(src.at[pl.ds(to, 1)], dst.at[pl.ds(me, 1)], send, recv, to).start()
+
+        far_first(go, 2)
+        dst[pl.ds(me, 1), :] = src[pl.ds(me, 1), :]
+
+    def gather_rows(row, dst, send, recv):
+        def go(to):
+            remote(row, dst.at[pl.ds(me, 1)], send, recv, to).start()
+
+        far_first(go, 2)
+        dst[pl.ds(me, 1), :] = row[...]
 
     build_onehot(onehot, rows_ref)
     scatter_sum(
         sums_b, left, onehot, rows_ref, signs_f,
         lambda c: tall[pl.ds(pl.multiple_of(c * COLUMNS, COLUMNS), COLUMNS), :], acc,
     )
-
-    def spread_rows(src, dst, send, recv):
-        def go(i):
-            to = peer(i)
-            remote(src.at[pl.ds(to, 1)], dst.at[pl.ds(me, 1)], send, recv, to).start()
-
-        each(peers, go)
-        dst[pl.ds(me, 1), :] = src[pl.ds(me, 1), :]
-
-    def gather_rows(row, dst, send, recv):
-        def go(i):
-            remote(row, dst.at[pl.ds(me, 1)], send, recv, peer(i)).start()
-
-        each(peers, go)
-        dst[pl.ds(me, 1), :] = row[...]
-
     spread_rows(sums_b, parts_b, rsb_s, rsb_r)
-
-    settle(in_box, mates * SENT, fwd_r)
-    for rho in range(4):
-        state_x[pl.ds(rho * LANES, LANES), :] = in_box[pl.ds(rho, CHIPS, stride=SLOT), :].T
-    point[...] = in_box[pl.ds(4, CHIPS, stride=SLOT), :].T
-    tail = in_box[pl.ds(5, CHIPS, stride=SLOT), :].T
-    signs_f[...] = tail[0:LEAF, :]
-    point_rows[...] = point[pl.ds(3 * LEAF, LEAF), :].astype(jnp.int32)
-    first[pl.ds(STATE, 2 * COLUMNS), :] = jnp.broadcast_to(
-        jnp.sum(tail[LEAF : LEAF + 2 * COLUMNS, :], axis=1, keepdims=True), (2 * COLUMNS, LANES)
-    )
-
-    size = 1.0 / math.sqrt(LEAF)
-    across = point[pl.ds(0, LEAF), :].astype(jnp.int32) * scale
-    down = point[pl.ds(LEAF, LEAF), :].astype(jnp.int32) * scale
-    turn_x = [turns(fold(across * f)) for f in range(1, 5)]
-    turn_y = [turns(fold(down * f)) for f in range(1, 5)]
-    for w in range(RANK):
-        c, s = both(turn_x[w % 4] + turn_y[w // 4], size)
-        for at, table in ((w, c), (w + RANK, s)):
-            leaf[pl.ds(at * LEAF, LEAF), :] = table
-            leaf_t[pl.ds(at, LEAF, stride=WIDTH), :] = table
-    combine(first, [(leaf_t, 0, state_x)])
+    send_slots(out_box, in_box, SENT, fwd_s, fwd_r)
+    group = lax.broadcasted_iota(jnp.int32, (8, LANES), 1) * CORES + core
+    lax.fori_loop(0, SECTIONS, make_sections(matrix, scale, group, chip), 0)
+
+    settle(in_c, mates * 4, coef_r)
+    for rho in range(4):
+        first[pl.ds(rho * LANES, LANES), :] = in_c[pl.ds(rho, CHIPS, stride=SLOT), :].T
 
     exchange = remote(first, first_p, ex_s, ex_r, other)
     exchange.start()
     combine(second, [(matrix, 0, first)])
-    build_onehot(onehot, point_rows)
     exchange.wait_recv()
     combine(second, [(matrix, WIDTH * WIDTH, first_p)], add=True)
     exchange.wait_send()
-
     source, target = second, first
     for k in range(1, SECTIONS):
         step = 1 << (k - 1)
 
         def swap(r, source=source, step=step):
-            at = pl.ds(pl.multiple_of(r * 64, 64), 64)
+            at = pl.ds(pl.multiple_of(r * 512, 512), 512)
             a = source[at, :]
             up = (lax.broadcasted_iota(jnp.int32, a.shape, 1) & step) != 0
             partner[at, :] = jnp.where(up, pltpu.roll(a, step, 1), pltpu.roll(a, LANES - step, 1))
 
-        each(STATE // 64, swap)
+        each(STATE // 512, swap)
         base = k * 2 * WIDTH * WIDTH
         combine(target, [(matrix, base, source), (matrix, base + WIDTH * WIDTH, partner)])
         source, target = target, source
@@ -380,12 +410,27 @@
             row_b[...] = jnp.sum(parts_b[...], axis=0, keepdims=True)
             gather_rows(row_b, all_b, agb_s, agb_r)
 
-    both_sums = first_p[pl.ds(STATE, 2 * COLUMNS), :] + half_mine_sum(first)
+    settle(in_box, mates * SENT, fwd_r)
+    tail = in_box[pl.ds(5, CHIPS, stride=SLOT), :].T
+    half_b[...] = jnp.broadcast_to(
+        jnp.sum(tail[LEAF : LEAF + 2 * COLUMNS, :], axis=1, keepdims=True), (2 * COLUMNS, LANES)
+    )
+    swap_b = remote(half_b, other_b, hb_s, hb_r, other)
+    swap_b.start()
+    signs_f[...] = tail[0:LEAF, :]
+    for rho in range(4):
+        state_x[pl.ds(rho * LANES, LANES), :] = in_box[pl.ds(rho, CHIPS, stride=SLOT), :].T
+    point[...] = in_box[pl.ds(4, CHIPS, stride=SLOT), :].T
+    point_rows[...] = point[pl.ds(3 * LEAF, LEAF), :].astype(jnp.int32)
+    leaf_tables(store_by_width)
+    build_onehot(onehot, point_rows)
+    combine(residual, [(leaf, 0, source)])
+    swap_b.wait()
+    both_sums = half_b[...] + other_b[...]
     total_b = both_sums[0:COLUMNS, :]
     total_db = both_sums[COLUMNS:, :]
     weight = total_b + EPSILON * TOTAL
     shift_rows[...] = total_db / weight
-    combine(residual, [(leaf, 0, source)])
     cross_sum = []
     square_sum = []
     for q in range(COLUMNS):
@@ -406,16 +451,7 @@
         out_back[pl.ds(rho, CHIPS, stride=SLOT), :] = residual[pl.ds(rho * LANES, LANES), :].T
     out_back[pl.ds(4, CHIPS, stride=SLOT), :] = jnp.broadcast_to(to_lanes(moments, 0), (CHIPS, LANES))
 
-    def send_back(i):
-        to = mate(i)
-        remote(
-            out_back.at[pl.ds(pl.multiple_of(SLOT * (to // CORES), SLOT), BACK)],
-            in_back.at[pl.ds(pl.multiple_of(SLOT * chip, SLOT), BACK)],
-            back_s, back_r, to,
-        ).start()
-
-    each(mates, send_back)
-    in_back[mine, :] = out_back[mine, :]
+    send_slots(out_back, in_back, BACK, back_s, back_r)
 
     settle(parts_r, peers, rs_r)
     row_r[...] = jnp.sum(parts_r[...], axis=0, keepdims=True)
@@ -454,6 +490,7 @@
         at = pl.ds(r, COLUMNS, stride=SKETCH // LANES)
         sketch_ref[:, r * LANES : (r + 1) * LANES] = (all_r[at, :] - delta * all_b[at, :]) * factor
 
+    settle(out_c, mates * 4, coef_s)
     settle(out_box, mates * SENT, fwd_s)
     settle(sums_b, peers, rsb_s)
     settle(all_b, peers, agb_s)
@@ -462,13 +499,10 @@
     settle(out_back, mates * BACK, back_s)
 
 
-def half_mine_sum(first):
-    return first[pl.ds(STATE, 2 * COLUMNS), :]
-
-
 def body(basis_vector, diagonal, coords, phase_scale, sketch_rows, sketch_signs):
     f32 = jnp.float32
     vmem = pl.BlockSpec(memory_space=pltpu.VMEM)
+    hbm = pl.BlockSpec(memory_space=pltpu.HBM)
     box_rows = CHIPS * SLOT
     scratch = [
         pltpu.VMEM((CHUNKS * COLUMNS, LANES), f32),
@@ -480,13 +514,17 @@
         pltpu.VMEM((WIDTH * LEAF, LANES), f32),
         pltpu.VMEM((WIDTH * LEAF, LANES), f32),
         pltpu.VMEM((STATE, LANES), f32),
-        pltpu.VMEM((STATE + 2 * COLUMNS, LANES), f32),
         pltpu.VMEM((STATE, LANES), f32),
-        pltpu.VMEM((STATE + 2 * COLUMNS, LANES), f32),
+        pltpu.VMEM((STATE, LANES), f32),
+        pltpu.VMEM((STATE, LANES), f32),
         pltpu.VMEM((STATE, LANES), f32),
         pltpu.VMEM((4 * LEAF, LANES), f32),
         pltpu.VMEM((LEAF, LANES), jnp.int32),
         pltpu.VMEM((STATE, LANES), f32),
+        pltpu.VMEM((box_rows, LANES), f32),
+        pltpu.VMEM((box_rows, LANES), f32),
+        pltpu.VMEM((2 * COLUMNS, LANES), f32),
+        pltpu.VMEM((2 * COLUMNS, LANES), f32),
         pltpu.VMEM((box_rows, LANES), f32),
         pltpu.VMEM((box_rows, LANES), f32),
         pltpu.VMEM((LOW, POINTS), jnp.bfloat16),
@@ -505,8 +543,14 @@
         pltpu.VMEM((8, LANES), f32),
         pltpu.VMEM((COLUMNS, LANES), f32),
         pltpu.VMEM((LEAF, LANES), f32),
+        pltpu.VMEM((COLUMNS, POINTS), f32),
+        pltpu.VMEM((CHUNKS, LANES), f32),
+        pltpu.VMEM((2, POINTS), jnp.int32),
+        pltpu.VMEM((CHUNKS, LANES), jnp.int32),
+        pltpu.VMEM((CHUNKS, LANES), jnp.int32),
+        pltpu.SemaphoreType.DMA((5,)),
     ]
-    scratch += [pltpu.SemaphoreType.DMA] * 16
+    scratch += [pltpu.SemaphoreType.DMA] * 20
     call = pl.pallas_call(
         kernel,
         out_shape=(
@@ -514,7 +558,7 @@
             jax.ShapeDtypeStruct((COLUMNS, SKETCH), f32),
             jax.ShapeDtypeStruct((2, COLUMNS), f32),
         ),
-        in_specs=[vmem, vmem, vmem, pl.BlockSpec(memory_space=pltpu.SMEM), vmem, vmem],
+        in_specs=[hbm, hbm, hbm, pl.BlockSpec(memory_space=pltpu.SMEM), hbm, hbm],
         out_specs=(vmem, vmem, vmem),
         scratch_shapes=scratch,
         compiler_params=pltpu.CompilerParams(collective_id=1, has_side_effects=True, vmem_limit_bytes=48 << 20),

time: 80 us -> 67.6 us (0.84)
  Pallas kernels: 72.6 us -> 60.2 us
    pallas_call x1, Pallas kernels: 72.6 us -> 60.2 us  [body(): call(basis_vector, diagonal.reshape(table), coords, phase_scale, sketch_r...]
where the time goes in v3:
time: 67.6 us; the launch traced here: 67.3 us
  Pallas kernels  60.2 us (89%)
  local copies, waits for them, and re-layouts  5.77 us (9%)
  between operations  1.3 us (2%)
    pallas_call x1, Pallas kernels, body(): call(basis_vector, diagonal.reshape(table), coords, phase_scale, sketch_r...  60.2 us
    unnamed x13, local copies, waits for them, and re-layouts  5.77 us

profile of v3, /device:TPU:1, one launch (start us, length us, event | category | flops | bytes accessed | tf_op | source)
XLA Modules:
  0.0 67.3 jit_solution(16481278363431322795)
XLA Ops:
  1.3 0.0 copy-start
  1.3 0.9 %copy-done = f32[16,4096]{1,0:T(8,128)S(1)} copy-done((f32[16,4096]{1,0:T(8,128)S(1)}, f32[16,4096]{1,0:T(8,128)}, u32[]{:S(2)}) %copy-start) | copy-done | bytes 262168
  2.2 0.0 copy-start.1
  2.2 0.8 %copy-done.1 = s32[2,4096]{1,0:T(2,128)S(1)} copy-done((s32[2,4096]{1,0:T(2,128)S(1)}, s32[2,4096]{1,0:T(2,128)}, u32[]{:S(2)}) %copy-start.1) | copy-done | bytes 32792
  3.0 0.0 copy-start.2
  3.0 0.7 %copy-done.2 = f32[4096]{0:T(1024)S(1)} copy-done((f32[4096]{0:T(1024)S(1)}, f32[4096]{0:T(1024)}, u32[]{:S(2)}) %copy-start.2) | copy-done | bytes 16408
  3.7 0.0 copy-start.3
  3.7 0.7 %copy-done.3 = s32[4096]{0:T(1024)S(1)} copy-done((s32[4096]{0:T(1024)S(1)}, s32[4096]{0:T(1024)}, u32[]{:S(2)}) %copy-start.3) | copy-done | bytes 16408
  4.4 0.0 copy-start.4
  4.4 0.7 %copy-done.4 = s32[4096]{0:T(1024)S(1)} copy-done((s32[4096]{0:T(1024)S(1)}, s32[4096]{0:T(1024)}, u32[]{:S(2)}) %copy-start.4) | copy-done | bytes 16408
  5.1 60.2 %shard_map.85 = (f32[16,4096]{1,0:T(8,128)S(1)}, f32[16,2048]{1,0:T(8,128)S(1)}, f32[2,16]{1,0:T(2,128)S(1)}) custom-call(f32[16,4096]{1,0:T(8,128)S(1)} %copy-done, f32[32,128]{1,0:T(8,128)S(1)} %bitcast.3, s32[2,4096]{1,0:T(2,128)S(1)} %copy-done.1, s32[1]{0:T(128)S(6)} %copy.12.scale_ref, s32[32,128]{1,0:T(8,128)S(1)} %bitcast.4, s32[32,128]{1,0:T(8,128)S(1)} %bitcast.5), custom_call_target="tpu_custom_call" | custom-call | tf_op jit(solution)/shard_map/pallas_call | solution.py:567
  65.3 0.7 %copy.13 = f32[16,4096]{1,0:T(8,128)} copy(f32[16,4096]{1,0:T(8,128)S(1)} %get-tuple-element.6) | data formatting | bytes 524288
  66.0 0.7 copy.14
  66.7 0.6 copy.15
Async XLA Ops:
  1.3 1.0 %copy-start = (f32[16,4096]{1,0:T(8,128)S(1)}, f32[16,4096]{1,0:T(8,128)}, u32[]{:S(2)}) copy-start(f32[16,4096]{1,0:T(8,128)} %basis_hbm.1) | copy-start | bytes 786436
  2.2 0.8 %copy-start.1 = (s32[2,4096]{1,0:T(2,128)S(1)}, s32[2,4096]{1,0:T(2,128)}, u32[]{:S(2)}) copy-start(s32[2,4096]{1,0:T(2,128)} %coords_hbm.1) | copy-start | bytes 98308
  3.0 0.7 %copy-start.2 = (f32[4096]{0:T(1024)S(1)}, f32[4096]{0:T(1024)}, u32[]{:S(2)}) copy-start(f32[4096]{0:T(1024)} %param.7) | copy-start | bytes 49156
  3.7 0.7 %copy-start.3 = (s32[4096]{0:T(1024)S(1)}, s32[4096]{0:T(1024)}, u32[]{:S(2)}) copy-start(s32[4096]{0:T(1024)} %param.10) | copy-start | bytes 49156
  4.4 0.7 %copy-start.4 = (s32[4096]{0:T(1024)S(1)}, s32[4096]{0:T(1024)}, u32[]{:S(2)}) copy-start(s32[4096]{0:T(1024)} %param.11) | copy-start | bytes 49156

commit v4 on v3

--- a/solution.py
+++ b/solution.py
@@ -103,11 +103,13 @@
     return jnp.sum(jnp.where(here, jnp.broadcast_to(row, shape), 0.0), axis=1, keepdims=True)
 
 
-def combine(out_ref, terms, add=False):
+def combine(out_ref, terms, add=False, only=None):
     group = 4
 
     def one_group(g, carry):
-        first = pl.multiple_of(g * group * WIDTH, group * WIDTH)
+        first = g * group * WIDTH
+        if only is None:
+            first = pl.multiple_of(first, group * WIDTH)
         if add:
             acc = [out_ref[pl.ds(first + 8 * i, 8), :] for i in range(4 * group)]
         else:
@@ -128,7 +130,10 @@
             out_ref[pl.ds(first + 8 * i, 8), :] = acc[i]
         return carry
 
-    lax.fori_loop(0, COLUMNS // group, one_group, 0)
+    if only is None:
+        lax.fori_loop(0, COLUMNS // group, one_group, 0)
+    else:
+        one_group(only, 0)
 
 
 def build_onehot(onehot_ref, rows_ref):
@@ -147,13 +152,13 @@
     lax.fori_loop(0, CHUNKS, one, 0, unroll=2)
 
 
-def scatter_sum(sums_ref, left_ref, onehot_ref, rows_ref, signs_ref, values, acc_ref):
+def scatter_sum(sums_ref, left_ref, onehot_ref, rows_ref, signs_ref, values, acc_ref, blocks=1):
     def one(c, carry):
         x = values(c) * jnp.broadcast_to(signs_ref[pl.ds(c, 1), :], (COLUMNS, LANES))
         high = (rows_ref[pl.ds(c, 1), :] >> 8).astype(jnp.float32)
         high = jnp.broadcast_to(high, (COLUMNS, LANES)).astype(jnp.bfloat16)
         zero_b = jnp.zeros((COLUMNS, LANES), jnp.bfloat16)
-        here = pl.ds(pl.multiple_of(c * LANES, LANES), LANES)
+        here = pl.ds(c * LANES if blocks > 1 else pl.multiple_of(c * LANES, LANES), LANES)
         pieces = []
         for _ in range(PIECES):
             piece = x.astype(jnp.bfloat16)
@@ -165,10 +170,17 @@
                 left_ref[pl.ds((i * HIGH + h) * COLUMNS, COLUMNS), here] = jnp.where(hit, piece, zero_b)
         return carry
 
-    lax.fori_loop(0, CHUNKS, one, 0, unroll=2)
-    acc_ref[...] = lax.dot_general(
-        left_ref[...], onehot_ref[...], (((1,), (1,)), ((), ())), preferred_element_type=jnp.float32
-    )
+    if blocks == 1:
+        lax.fori_loop(0, CHUNKS, one, 0, unroll=2)
+    for block in range(blocks):
+        if blocks > 1:
+            for c in range(block * CHUNKS // blocks, (block + 1) * CHUNKS // blocks):
+                one(c, 0)
+        at = slice(block * POINTS // blocks, (block + 1) * POINTS // blocks)
+        part = lax.dot_general(
+            left_ref[:, at], onehot_ref[:, at], (((1,), (1,)), ((), ())), preferred_element_type=jnp.float32
+        )
+        acc_ref[...] = part if block == 0 else acc_ref[...] + part
     rows = HIGH * COLUMNS
     total = acc_ref[pl.ds(0, rows), :] + acc_ref[pl.ds(rows, rows), :]
     for h in range(HIGH):
@@ -233,21 +245,22 @@
     x = lax.rem(chip, 4)
     z = lax.rem(me // 8, 8)
     y = me // 64
-    x_at = [lax.rem(x + i, 4) * 2 for i in range(4)]
-    y_at = [lax.rem(y + i, 4) * 64 for i in range(4)]
+    x_at = [lax.rem(x + i, 4) for i in range(4)]
+    y_at = [lax.rem(y + i, 4) * 32 for i in range(4)]
     core_at = [core, 1 - core]
 
     def far_first(what, cores):
         steps = [(a, b, c) for a in range(4) for b in range(4) for c in range(cores)]
         steps.sort(key=lambda s: -(min(s[0], 4 - s[0]) + min(s[1], 4 - s[1]) + 0.1 * s[2]))
-        near = [[y_at[a] + x_at[b] + core_at[c] for b in range(4)] for a in range(4) for c in range(cores)]
+        near = [[y_at[a] + x_at[b] for b in range(4)] for a in range(4)]
 
         def layer(dz, own):
-            base = lax.rem(z + dz, 8) * 8
+            base = lax.rem(z + dz, 8) * 4
             for a, b, c in steps:
                 if own and (a, b, c) == (0, 0, 0):
                     continue
-                what(near[a * cores + c][b] + base)
+                place = near[a][b] + base
+                what(place, place * CORES + core_at[c])
 
         def body(i, carry):
             layer(4 + ((i + 1) // 2) * (1 - 2 * lax.rem(i, 2)), False)
@@ -277,7 +290,7 @@
     ):
         loads.append(pltpu.make_async_copy(src, dst, load_sem.at[i]))
         loads[-1].start()
-    far_first(lambda to: pl.semaphore_signal(barrier, inc=1, device_id=(to,), device_id_type=MESH), 2)
+    far_first(lambda place, to: pl.semaphore_signal(barrier, inc=1, device_id=(to,), device_id_type=MESH), 2)
     for load in loads:
         load.wait()
 
@@ -344,9 +357,9 @@
     pl.semaphore_wait(barrier, peers)
 
     def send_slots(src, dst, count, send, recv):
-        def go(to):
+        def go(place, to):
             remote(
-                src.at[pl.ds(pl.multiple_of(SLOT * (to // CORES), SLOT), count)],
+                src.at[pl.ds(pl.multiple_of(SLOT * place, SLOT), count)],
                 dst.at[pl.ds(pl.multiple_of(SLOT * chip, SLOT), count)],
                 send, recv, to,
             ).start()
@@ -358,14 +371,14 @@
     send_slots(out_c, in_c, 4, coef_s, coef_r)
 
     def spread_rows(src, dst, send, recv):
-        def go(to):
+        def go(place, to):
             remote(src.at[pl.ds(to, 1)], dst.at[pl.ds(me, 1)], send, recv, to).start()
 
         far_first(go, 2)
         dst[pl.ds(me, 1), :] = src[pl.ds(me, 1), :]
 
     def gather_rows(row, dst, send, recv):
-        def go(to):
+        def go(place, to):
             remote(row, dst.at[pl.ds(me, 1)], send, recv, to).start()
 
         far_first(go, 2)
@@ -385,12 +398,16 @@
     for rho in range(4):
         first[pl.ds(rho * LANES, LANES), :] = in_c[pl.ds(rho, CHIPS, stride=SLOT), :].T
 
-    exchange = remote(first, first_p, ex_s, ex_r, other)
-    exchange.start()
+    pieces = [pl.ds(rho * LANES, LANES) for rho in range(4)]
+    exchange = [remote(first.at[at], first_p.at[at], ex_s.at[i], ex_r.at[i], other) for i, at in enumerate(pieces)]
+    for piece in exchange:
+        piece.start()
     combine(second, [(matrix, 0, first)])
-    exchange.wait_recv()
-    combine(second, [(matrix, WIDTH * WIDTH, first_p)], add=True)
-    exchange.wait_send()
+    for i, piece in enumerate(exchange):
+        piece.wait_recv()
+        combine(second, [(matrix, WIDTH * WIDTH, first_p)], add=True, only=i)
+    for piece in exchange:
+        piece.wait_send()
     source, target = second, first
     for k in range(1, SECTIONS):
         step = 1 << (k - 1)
@@ -405,7 +422,7 @@
         base = k * 2 * WIDTH * WIDTH
         combine(target, [(matrix, base, source), (matrix, base + WIDTH * WIDTH, partner)])
         source, target = target, source
-        if k == 2:
+        if k == 5:
             settle(parts_b, peers, rsb_r)
             row_b[...] = jnp.sum(parts_b[...], axis=0, keepdims=True)
             gather_rows(row_b, all_b, agb_s, agb_r)
@@ -443,7 +460,7 @@
     moments = jnp.sum(jnp.concatenate(cross_sum + square_sum, axis=0), axis=1, keepdims=True)
     scatter_sum(
         sums_r, left, onehot, point_rows, signs_f,
-        lambda c: residual[pl.ds(c, COLUMNS, stride=LEAF), :], acc,
+        lambda c: residual[pl.ds(c, COLUMNS, stride=LEAF), :], acc, blocks=4,
     )
     spread_rows(sums_r, parts_r, rs_s, rs_r)
 
@@ -484,19 +501,34 @@
         new_ref[:, c * LANES : (c + 1) * LANES] = (flat_x[at, :] - delta * tall[at, :]) * inverse
 
     settle(all_b, peers, agb_r)
-    settle(all_r, peers, ag_r)
     factor = inverse * math.sqrt(SKETCH / TOTAL)
+    shift = delta * factor
     for r in range(SKETCH // LANES):
         at = pl.ds(r, COLUMNS, stride=SKETCH // LANES)
-        sketch_ref[:, r * LANES : (r + 1) * LANES] = (all_r[at, :] - delta * all_b[at, :]) * factor
-
+        sketch_ref[:, r * LANES : (r + 1) * LANES] = shift * all_b[at, :]
     settle(out_c, mates * 4, coef_s)
     settle(out_box, mates * SENT, fwd_s)
     settle(sums_b, peers, rsb_s)
     settle(all_b, peers, agb_s)
     settle(sums_r, peers, rs_s)
+    settle(out_back, mates * BACK, back_s)
+    settle(all_r, peers, ag_r)
+    for r in range(SKETCH // LANES):
+        at = pl.ds(r, COLUMNS, stride=SKETCH // LANES)
+        here = slice(r * LANES, (r + 1) * LANES)
+        sketch_ref[:, here] = all_r[at, :] * factor - sketch_ref[:, here]
     settle(all_r, peers, ag_s)
-    settle(out_back, mates * BACK, back_s)
+
+
+def put(new_ref, sketch_ref, arnoldi_ref, new_hbm, sketch_hbm, arnoldi_hbm, sems):
+    copies = [
+        pltpu.make_async_copy(src, dst, sems.at[i])
+        for i, (src, dst) in enumerate(((new_ref, new_hbm), (sketch_ref, sketch_hbm), (arnoldi_ref, arnoldi_hbm)))
+    ]
+    for copy in copies:
+        copy.start()
+    for copy in copies:
+        copy.wait()
 
 
 def body(basis_vector, diagonal, coords, phase_scale, sketch_rows, sketch_signs):
@@ -550,21 +582,22 @@
         pltpu.VMEM((CHUNKS, LANES), jnp.int32),
         pltpu.SemaphoreType.DMA((5,)),
     ]
-    scratch += [pltpu.SemaphoreType.DMA] * 20
+    scratch += [pltpu.SemaphoreType.DMA] * 2 + [pltpu.SemaphoreType.DMA((4,))] * 2 + [pltpu.SemaphoreType.DMA] * 16
+    results = (
+        jax.ShapeDtypeStruct((COLUMNS, POINTS), f32),
+        jax.ShapeDtypeStruct((COLUMNS, SKETCH), f32),
+        jax.ShapeDtypeStruct((2, COLUMNS), f32),
+    )
     call = pl.pallas_call(
         kernel,
-        out_shape=(
-            jax.ShapeDtypeStruct((COLUMNS, POINTS), f32),
-            jax.ShapeDtypeStruct((COLUMNS, SKETCH), f32),
-            jax.ShapeDtypeStruct((2, COLUMNS), f32),
-        ),
+        out_shape=results,
         in_specs=[hbm, hbm, hbm, pl.BlockSpec(memory_space=pltpu.SMEM), hbm, hbm],
         out_specs=(vmem, vmem, vmem),
         scratch_shapes=scratch,
         compiler_params=pltpu.CompilerParams(collective_id=1, has_side_effects=True, vmem_limit_bytes=48 << 20),
     )
     table = (CHUNKS, LANES)
-    return call(
+    inputs = (
         basis_vector,
         diagonal.reshape(table),
         coords,
@@ -572,6 +605,15 @@
         sketch_rows.reshape(table),
         sketch_signs.reshape(table),
     )
+    found = call(*[x if x is phase_scale else pltpu.with_memory_space_constraint(x, pltpu.HBM) for x in inputs])
+    return pl.pallas_call(
+        put,
+        out_shape=results,
+        in_specs=[vmem] * 3,
+        out_specs=(hbm,) * 3,
+        scratch_shapes=[pltpu.SemaphoreType.DMA((3,))],
+        compiler_params=pltpu.CompilerParams(vmem_limit_bytes=4 << 20),
+    )(*found)
 
 
 def solution(mesh):

time: 67.6 us -> 60.9 us (0.901)
  local copies, waits for them, and re-layouts: 5.77 us -> 0 us
  Pallas kernels: 60.2 us -> 59.5 us
    unnamed x13 -> x0, local copies, waits for them, and re-layouts: 5.77 us -> none
    pallas_call x1 -> x2, Pallas kernels: 60.2 us -> 59.5 us  [the longest x1 58.7 us: body(): call(*[x if x is phase_scale else pltpu.with_memory_space_constraint(x, p...]
where the time goes in v4:
time: 60.9 us; the launch traced here: 60.8 us
  Pallas kernels  59.5 us (98%)
  between operations  1.29 us (2%)
    pallas_call x1, Pallas kernels, body(): call(*[x if x is phase_scale else pltpu.with_memory_space_constraint(x, p...  58.7 us

profile of v4, /device:TPU:1, one launch (start us, length us, event | category | flops | bytes accessed | tf_op | source)
XLA Modules:
  0.0 60.8 jit_solution(8633154816923899948)
XLA Ops:
  1.3 58.7 %shard_map.85 = (f32[16,4096]{1,0:T(8,128)S(1)}, f32[16,2048]{1,0:T(8,128)S(1)}, f32[2,16]{1,0:T(2,128)S(1)}) custom-call(f32[16,4096]{1,0:T(8,128)} %basis_hbm.1, f32[32,128]{1,0:T(8,128)} %bitcast.3, s32[2,4096]{1,0:T(2,128)} %coords_hbm.1, s32[1]{0:T(128)S(6)} %copy.9.scale_ref, s32[32,128]{1,0:T(8,128)} %bitcast.4, s32[32,128]{1,0:T(8,128)} %bitcast.5), custom_call_target="tpu_custom_call" | custom-call | tf_op jit(solution)/shard_map/pallas_call | solution.py:608
  60.0 0.8 %shard_map.86 = (f32[16,4096]{1,0:T(8,128)}, f32[16,2048]{1,0:T(8,128)}, f32[2,16]{1,0:T(2,128)}) custom-call(f32[16,4096]{1,0:T(8,128)S(1)} %get-tuple-element.6.new_ref, f32[16,2048]{1,0:T(8,128)S(1)} %get-tuple-element.7.sketch_ref, f32[2,16]{1,0:T(2,128)S(1)} %get-tuple-element.8.arnoldi_ref), custom_call_target="tpu_custom_call" | custom-call | tf_op jit(solution)/shard_map/pallas_call | solution.py:609

commit v5 on v4

--- a/solution.py
+++ b/solution.py
@@ -26,6 +26,8 @@
 MODULUS = 8191
 EPSILON = 1e-06
 SLOT = 8
+TILES = 16
+QUIET = 4
 SENT = 6
 BACK = 5
 LOW = 256
@@ -189,37 +191,75 @@
             sums_ref[pl.ds(h * (LOW // LANES) + half, COLUMNS, stride=SKETCH // LANES), :] = block
 
 
-def make_sections(matrix_ref, scale, group, chip):
+def make_units(own_ref, cross_ref, scale, core, chip):
+    lane = lax.broadcasted_iota(jnp.int32, (8, LANES), 1)
+    sub = lax.broadcasted_iota(jnp.int32, (8, LANES), 0)
+    v = lax.rem(lane, WIDTH)
+    for part in range(4):
+        mate = 4 * (8 * part + sub) + lane // WIDTH
+        box = (mate * CORES + core) * BOXES + chip
+        start = lax.rem(box * 37, MODULUS - 1)
+        for k in range(SECTIONS):
+            key = start + 101 * k
+            key = jnp.where(key >= MODULUS - 1, key - (MODULUS - 1), key)
+            unit = fold(scale * (key + 1))
+            cross = (v + 1) * unit
+            here = pl.ds(k * 2 * TILES + 8 * part, 8)
+            own_ref[here, :] = turns(fold(cross + unit))
+            cross_ref[here, :] = turns(fold(cross))
+
+
+def make_sections(matrix_ref, own_ref, cross_ref):
     own_size = 0.35 / math.sqrt(WIDTH)
     cross_size = 0.6 / math.sqrt(WIDTH)
     sub = lax.broadcasted_iota(jnp.int32, (8, LANES), 0)
-    box = group * BOXES + chip
-
-    def one(k, carry):
-        key = box * 37 + 101 * k
-        guess = (key.astype(jnp.float32) * jnp.float32(1.0 / (MODULUS - 1))).astype(jnp.int32)
-        key = key - guess * (MODULUS - 1)
-        key = jnp.where(key < 0, key + (MODULUS - 1), key)
-        key = jnp.where(key >= MODULUS - 1, key - (MODULUS - 1), key)
-        unit = fold(scale * (key + 1))
-        base = pl.multiple_of(k * (2 * WIDTH * WIDTH), 2 * WIDTH * WIDTH)
+    square = (WIDTH, LANES)
+    same = lax.broadcasted_iota(jnp.int32, square, 0) == lax.rem(lax.broadcasted_iota(jnp.int32, square, 1), WIDTH)
+    ident = jnp.where(same, 0.85, 0.0)
+
+    def one(i):
+        rows = pl.multiple_of(i * 2 * WIDTH, 2 * WIDTH)
         half = turns(jnp.int32(4096))
-        for t in range(4):
-            own_step = turns(fold((sub + (8 * t + 1)) * unit))
-            cross_step = turns(fold((sub + (8 * t + 3)) * unit))
-            own_turn = own_step
-            cross_turn = jnp.broadcast_to(half, (8, LANES))
-            for v in range(WIDTH):
-                own_turn = own_turn + own_step
-                cross_turn = cross_turn + cross_step
-                own = cosine(own_turn, own_size)
-                if v // 8 == t:
-                    own = own + jnp.where(sub == v % 8, 0.85, 0.0)
-                matrix_ref[pl.ds(base + v * WIDTH + 8 * t, 8), :] = own
-                matrix_ref[pl.ds(base + WIDTH * WIDTH + v * WIDTH + 8 * t, 8), :] = cosine(cross_turn, cross_size)
-        return carry
+        for t in range(2):
+            own_unit = own_ref[pl.ds(2 * i + t, 8, stride=0), :]
+            cross_unit = cross_ref[pl.ds(2 * i + t, 8, stride=0), :]
+            own_turn = (sub + 1) * own_unit
+            cross_turn = (sub + 3) * cross_unit + half
+            own_rows, cross_rows = [], []
+            for _ in range(4):
+                own_rows.append(cosine(own_turn, own_size))
+                cross_rows.append(cosine(cross_turn, cross_size))
+                own_turn = own_turn + (own_unit << 3)
+                cross_turn = cross_turn + (cross_unit << 3)
+            own = jnp.concatenate(own_rows, axis=0) + ident
+            cross = jnp.concatenate(cross_rows, axis=0)
+            for part, value in ((0, own), (1, cross)):
+                here = pl.ds((2 * part + t) * LANES, LANES)
+                high = value.astype(jnp.bfloat16)
+                matrix_ref[pl.ds(rows, WIDTH), here] = high
+                matrix_ref[pl.ds(rows + WIDTH, WIDTH), here] = (value - high.astype(jnp.float32)).astype(jnp.bfloat16)
 
     return one
+
+
+def weights(x):
+    box = lax.broadcasted_iota(jnp.int32, x.shape, 1)
+    box = (lax.rem(box, 32) // 4).astype(jnp.float32).astype(jnp.bfloat16)
+    zero = jnp.zeros(x.shape, jnp.bfloat16)
+    high = x.astype(jnp.bfloat16)
+    low = (x - high.astype(jnp.float32)).astype(jnp.bfloat16)
+    return jnp.concatenate(
+        [
+            jnp.concatenate([jnp.where(box == jnp.full(x.shape, b, jnp.bfloat16), y, zero) for b in range(8)], axis=0)
+            for y in (high, low)
+        ],
+        axis=1,
+    )
+
+
+def three_products(left, right):
+    r = lax.dot_general(left, right, (((1,), (0,)), ((), ())), preferred_element_type=jnp.float32)
+    return r[0:WIDTH, 0:LANES] + r[0:WIDTH, LANES:] + r[WIDTH:, 0:LANES]
 
 
 def kernel(
@@ -230,7 +270,7 @@
     out_c, in_c, half_b, other_b,
     out_back, in_back, onehot, left, acc, sums_b, parts_b, row_b, all_b, sums_r, parts_r, row_r, all_r,
     half_mine, half_other, shift_rows, signs_f,
-    basis_ref, diag_ref, coords_ref, rows_ref, signs_ref, load_sem,
+    basis_ref, diag_ref, coords_ref, rows_ref, signs_ref, own_units, cross_units, load_sem,
     fwd_s, fwd_r, ex_s, ex_r, rsb_s, rsb_r, agb_s, agb_r, rs_s, rs_r, ag_s, ag_r, back_s, back_r, mom_s, mom_r,
     coef_s, coef_r, hb_s, hb_r,
 ):
@@ -352,80 +392,137 @@
     leaf_tables(store_by_point)
     combine(second, [(leaf_t, 0, state_x)])
     for rho in range(4):
-        out_c[pl.ds(rho, CHIPS, stride=SLOT), :] = second[pl.ds(rho * LANES, LANES), :].T
-
-    pl.semaphore_wait(barrier, peers)
-
-    def send_slots(src, dst, count, send, recv):
-        def go(place, to):
-            remote(
-                src.at[pl.ds(pl.multiple_of(SLOT * place, SLOT), count)],
-                dst.at[pl.ds(pl.multiple_of(SLOT * chip, SLOT), count)],
-                send, recv, to,
-            ).start()
-
-        far_first(go, 1)
-        mine = pl.ds(pl.multiple_of(SLOT * chip, SLOT), count)
-        dst[mine, :] = src[mine, :]
-
-    send_slots(out_c, in_c, 4, coef_s, coef_r)
-
-    def spread_rows(src, dst, send, recv):
-        def go(place, to):
-            remote(src.at[pl.ds(to, 1)], dst.at[pl.ds(me, 1)], send, recv, to).start()
-
-        far_first(go, 2)
-        dst[pl.ds(me, 1), :] = src[pl.ds(me, 1), :]
-
-    def gather_rows(row, dst, send, recv):
-        def go(place, to):
-            remote(row, dst.at[pl.ds(me, 1)], send, recv, to).start()
-
-        far_first(go, 2)
-        dst[pl.ds(me, 1), :] = row[...]
+        out_c[pl.ds(rho, CHIPS, stride=4), :] = second[pl.ds(rho * LANES, LANES), :].T
 
     build_onehot(onehot, rows_ref)
     scatter_sum(
         sums_b, left, onehot, rows_ref, signs_f,
         lambda c: tall[pl.ds(pl.multiple_of(c * COLUMNS, COLUMNS), COLUMNS), :], acc,
     )
-    spread_rows(sums_b, parts_b, rsb_s, rsb_r)
-    send_slots(out_box, in_box, SENT, fwd_s, fwd_r)
-    group = lax.broadcasted_iota(jnp.int32, (8, LANES), 1) * CORES + core
-    lax.fori_loop(0, SECTIONS, make_sections(matrix, scale, group, chip), 0)
+    make_units(own_units, cross_units, scale, core, chip)
+    section = make_sections(matrix, own_units, cross_units)
+    pl.semaphore_wait(barrier, peers)
+
+    def send_slots(src, dst, count, send, recv, slot=SLOT):
+        def go(place, to):
+            remote(
+                src.at[pl.ds(pl.multiple_of(slot * place, slot), count)],
+                dst.at[pl.ds(pl.multiple_of(slot * chip, slot), count)],
+                send, recv, to,
+            ).start()
+
+        far_first(go, 1)
+        mine = pl.ds(pl.multiple_of(slot * chip, slot), count)
+        dst[mine, :] = src[mine, :]
+
+    send_slots(out_c, in_c, 4, coef_s, coef_r, slot=4)
+
+    def spread_rows(src, dst, send, recv):
+        def go(place, to):
+            remote(src.at[pl.ds(to, 1)], dst.at[pl.ds(me, 1)], send, recv, to).start()
+
+        far_first(go, 2)
+        dst[pl.ds(me, 1), :] = src[pl.ds(me, 1), :]
+
+    def gather_rows(row, dst, send, recv):
+        def go(place, to):
+            remote(row, dst.at[pl.ds(me, 1)], send, recv, to).start()
+
+        far_first(go, 2)
+        dst[pl.ds(me, 1), :] = row[...]
+
+    def send_sums(to):
+        remote(sums_b.at[pl.ds(to, 1)], parts_b.at[pl.ds(me, 1)], rsb_s, rsb_r, to).start()
+
+    def send_points(place):
+        remote(
+            out_box.at[pl.ds(pl.multiple_of(SLOT * place, SLOT), SENT)],
+            in_box.at[pl.ds(pl.multiple_of(SLOT * chip, SLOT), SENT)],
+            fwd_s, fwd_r, place * CORES + core,
+        ).start()
+
+    def pair(i):
+        section(2 * i)
+        section(2 * i + 1)
+
+    def at_step(offset):
+        return lax.rem(chip + offset, CHIPS)
+
+    def quiet(i, carry):
+        pair(i)
+        return carry
+
+    def with_points(i, carry):
+        for n in range(4):
+            send_points(at_step(4 * i + n + 1))
+        pair(QUIET + i)
+        return carry
+
+    def with_sums(i, carry):
+        for n in range(8):
+            send_sums(at_step(8 * i + n + 1) * CORES)
+            send_sums(at_step(8 * i + n + 1) * CORES + 1)
+        pair(QUIET + 32 + i)
+        return carry
+
+    lax.fori_loop(0, QUIET, quiet, 0)
+    lax.fori_loop(0, 31, with_points, 0)
+    for n in range(3):
+        send_points(at_step(125 + n))
+    pair(QUIET + 31)
+    mine = pl.ds(pl.multiple_of(SLOT * chip, SLOT), SENT)
+    in_box[mine, :] = out_box[mine, :]
+    lax.fori_loop(0, 15, with_sums, 0)
+    for n in range(7):
+        send_sums(at_step(121 + n) * CORES)
+        send_sums(at_step(121 + n) * CORES + 1)
+    send_sums(other)
+    parts_b[pl.ds(me, 1), :] = sums_b[pl.ds(me, 1), :]
+    for i in range(QUIET + 47, 64):
+        pair(i)
 
     settle(in_c, mates * 4, coef_r)
-    for rho in range(4):
-        first[pl.ds(rho * LANES, LANES), :] = in_c[pl.ds(rho, CHIPS, stride=SLOT), :].T
+    for quarter in range(4):
+        turned = in_c[pl.ds(quarter * LANES, LANES), :].T
+        tiles = swap_groups([turned[j * WIDTH : (j + 1) * WIDTH, :] for j in range(4)])
+        for i in range(4):
+            first[pl.ds((4 * quarter + i) * WIDTH, WIDTH), :] = tiles[i]
 
     pieces = [pl.ds(rho * LANES, LANES) for rho in range(4)]
     exchange = [remote(first.at[at], first_p.at[at], ex_s.at[i], ex_r.at[i], other) for i, at in enumerate(pieces)]
     for piece in exchange:
         piece.start()
-    combine(second, [(matrix, 0, first)])
-    for i, piece in enumerate(exchange):
-        piece.wait_recv()
-        combine(second, [(matrix, WIDTH * WIDTH, first_p)], add=True, only=i)
-    for piece in exchange:
-        piece.wait_send()
-    source, target = second, first
-    for k in range(1, SECTIONS):
-        step = 1 << (k - 1)
-
-        def swap(r, source=source, step=step):
-            at = pl.ds(pl.multiple_of(r * 512, 512), 512)
-            a = source[at, :]
-            up = (lax.broadcasted_iota(jnp.int32, a.shape, 1) & step) != 0
-            partner[at, :] = jnp.where(up, pltpu.roll(a, step, 1), pltpu.roll(a, LANES - step, 1))
-
-        each(STATE // 512, swap)
-        base = k * 2 * WIDTH * WIDTH
-        combine(target, [(matrix, base, source), (matrix, base + WIDTH * WIDTH, partner)])
-        source, target = target, source
-        if k == 5:
-            settle(parts_b, peers, rsb_r)
-            row_b[...] = jnp.sum(parts_b[...], axis=0, keepdims=True)
-            gather_rows(row_b, all_b, agb_s, agb_r)
+
+    def rows_of(tile):
+        return pl.ds(tile * WIDTH, WIDTH)
+
+    for k in range(SECTIONS):
+        source, target = (first, second) if k % 2 == 0 else (second, first)
+        if k == 1:
+            for piece in exchange:
+                piece.wait_send()
+        for tile in range(TILES):
+            x = source[rows_of(tile), :]
+            if k == 0:
+                if tile % 4 == 0:
+                    exchange[tile // 4].wait_recv()
+                y = first_p[rows_of(tile), :]
+            elif k < 4:
+                step = 4 << (k - 1)
+                up = (lax.broadcasted_iota(jnp.int32, x.shape, 1) & step) != 0
+                y = jnp.where(up, pltpu.roll(x, step, 1), pltpu.roll(x, LANES - step, 1))
+            else:
+                y = source[rows_of(tile ^ (1 << (k - 4))), :]
+            left_rows = matrix[pl.ds((k * TILES + tile) * 2 * WIDTH, 2 * WIDTH), :]
+            right = jnp.concatenate([weights(x), weights(y)], axis=0)
+            target[rows_of(tile), :] = three_products(left_rows, right)
+
+    for quarter in range(4):
+        parts = swap_groups([first[rows_of(4 * quarter + i), :] for i in range(4)])
+        second[pl.ds(quarter * LANES, LANES), :] = jnp.concatenate(parts, axis=0).T
+    for rho in range(4):
+        partner[pl.ds(rho * LANES, LANES), :] = second[pl.ds(rho, CHIPS, stride=4), :].T
+    source = partner
 
     settle(in_box, mates * SENT, fwd_r)
     tail = in_box[pl.ds(5, CHIPS, stride=SLOT), :].T
@@ -470,6 +567,10 @@
 
     send_slots(out_back, in_back, BACK, back_s, back_r)
 
+    settle(parts_b, peers, rsb_r)
+    row_b[...] = jnp.sum(parts_b[...], axis=0, keepdims=True)
+    gather_rows(row_b, all_b, agb_s, agb_r)
+
     settle(parts_r, peers, rs_r)
     row_r[...] = jnp.sum(parts_r[...], axis=0, keepdims=True)
     gather_rows(row_r, all_r, ag_s, ag_r)
@@ -542,7 +643,7 @@
         pltpu.VMEM((CHUNKS * COLUMNS, LANES), f32),
         pltpu.VMEM((box_rows, LANES), f32),
         pltpu.VMEM((box_rows, LANES), f32),
-        pltpu.VMEM((SECTIONS * 2 * WIDTH * WIDTH, LANES), f32),
+        pltpu.VMEM((SECTIONS * TILES * 2 * WIDTH, 4 * LANES), jnp.bfloat16),
         pltpu.VMEM((WIDTH * LEAF, LANES), f32),
         pltpu.VMEM((WIDTH * LEAF, LANES), f32),
         pltpu.VMEM((STATE, LANES), f32),
@@ -553,8 +654,8 @@
         pltpu.VMEM((4 * LEAF, LANES), f32),
         pltpu.VMEM((LEAF, LANES), jnp.int32),
         pltpu.VMEM((STATE, LANES), f32),
-        pltpu.VMEM((box_rows, LANES), f32),
-        pltpu.VMEM((box_rows, LANES), f32),
+        pltpu.VMEM((CHIPS * 4, LANES), f32),
+        pltpu.VMEM((CHIPS * 4, LANES), f32),
         pltpu.VMEM((2 * COLUMNS, LANES), f32),
         pltpu.VMEM((2 * COLUMNS, LANES), f32),
         pltpu.VMEM((box_rows, LANES), f32),
@@ -580,6 +681,8 @@
         pltpu.VMEM((2, POINTS), jnp.int32),
         pltpu.VMEM((CHUNKS, LANES), jnp.int32),
         pltpu.VMEM((CHUNKS, LANES), jnp.int32),
+        pltpu.VMEM((2 * SECTIONS * TILES + 8, LANES), jnp.int32),
+        pltpu.VMEM((2 * SECTIONS * TILES + 8, LANES), jnp.int32),
         pltpu.SemaphoreType.DMA((5,)),
     ]
     scratch += [pltpu.SemaphoreType.DMA] * 2 + [pltpu.SemaphoreType.DMA((4,))] * 2 + [pltpu.SemaphoreType.DMA] * 16

time: 60.9 us -> 60 us (0.985)
  Pallas kernels: 59.5 us -> 58.6 us
    pallas_call x1, Pallas kernels: 58.7 us -> 57.8 us  [body(): call(*[x if x is phase_scale else pltpu.with_memory_space_constraint(x, p...]
where the time goes in v5:
time: 60 us; the launch traced here: 59.9 us
  Pallas kernels  58.6 us (98%)
  between operations  1.29 us (2%)
    pallas_call x1, Pallas kernels, body(): call(*[x if x is phase_scale else pltpu.with_memory_space_constraint(x, p...  57.8 us

profile of v5, /device:TPU:1, one launch (start us, length us, event | category | flops | bytes accessed | tf_op | source)
XLA Modules:
  0.0 59.9 jit_solution(6871610795735006910)
XLA Ops:
  1.3 57.8 %shard_map.85 = (f32[16,4096]{1,0:T(8,128)S(1)}, f32[16,2048]{1,0:T(8,128)S(1)}, f32[2,16]{1,0:T(2,128)S(1)}) custom-call(f32[16,4096]{1,0:T(8,128)} %basis_hbm.1, f32[32,128]{1,0:T(8,128)} %bitcast.3, s32[2,4096]{1,0:T(2,128)} %coords_hbm.1, s32[1]{0:T(128)S(6)} %copy.9.scale_ref, s32[32,128]{1,0:T(8,128)} %bitcast.4, s32[32,128]{1,0:T(8,128)} %bitcast.5), custom_call_target="tpu_custom_call" | custom-call | tf_op jit(solution)/shard_map/pallas_call | solution.py:711
  59.1 0.8 %shard_map.86 = (f32[16,4096]{1,0:T(8,128)}, f32[16,2048]{1,0:T(8,128)}, f32[2,16]{1,0:T(2,128)}) custom-call(f32[16,4096]{1,0:T(8,128)S(1)} %get-tuple-element.6.new_ref, f32[16,2048]{1,0:T(8,128)S(1)} %get-tuple-element.7.sketch_ref, f32[2,16]{1,0:T(2,128)S(1)} %get-tuple-element.8.arnoldi_ref), custom_call_target="tpu_custom_call" | custom-call | tf_op jit(solution)/shard_map/pallas_call | solution.py:712
